TPU v7x, 128 devices: a whole 4x4x4 slice. The times are simulated.
128 devices in a mesh: dp: 8 (over z_hi, y), tensor: 16 (over x, z_lo, core).
Axes of the slice: x: 4, y: 4, z: 4 (z_hi: 2, z_lo: 2; z = z_hi * 2 + z_lo), core: 2. Of those that a mesh axis runs over, the one named last changes fastest.
Arguments:
- noisy: bfloat16 [64, 256, 1152], P('dp', None, 'tensor'), may hold values from -6 to 6
- labels: int32 [64], P('dp'), may hold values from 0 to 999
- tsteps: int32 [64], P('dp'), may hold values from 0 to 999
- guide_index: int32 [64], P('dp'), may hold values from 0 to 31
- class_table: bfloat16 [1001, 1152], replicated, may hold values from -6 to 6
- time_table: bfloat16 [1000, 1152], replicated, may hold values from -6 to 6
- guide_table: bfloat16 [32, 1152], replicated, may hold values from -6 to 6
- guide_weights: float32 [32], replicated, may hold values from 0.5 to 4
- teacher_qkv: bfloat16 [1152, 3456], P(None, 'tensor'), may hold values from -0.1875 to 0.1875
- teacher_out: bfloat16 [1152, 1152], P('tensor'), may hold values from -0.1875 to 0.1875
- teacher_ada: bfloat16 [3, 1152, 1152], P(None, None, 'tensor'), may hold values from -0.1875 to 0.1875
- student_qkv: bfloat16 [1152, 3456], P(None, 'tensor'), may hold values from -0.1875 to 0.1875
- student_out: bfloat16 [1152, 1152], P('tensor'), may hold values from -0.1875 to 0.1875
- student_ada: bfloat16 [3, 1152, 1152], P(None, None, 'tensor'), may hold values from -0.1875 to 0.1875
Outputs:
- grad_qkv: float32 [1152, 3456], P('dp', 'tensor')
- grad_out: float32 [1152, 1152], P('tensor', 'dp')
- grad_ada: float32 [3, 1152, 1152], P(None, 'dp', 'tensor')
All inputs are finite; a program needn't handle non-finite values.
Results may differ from a plain program's by a relative error of at most 0.034.
Values may be sent and summed in bfloat16 or wider, within the bound.
A program may use at most 128 MiB of HBM per device.

v0:
```python
import math

import jax
import jax.numpy as jnp
from jax import lax
from jax.sharding import PartitionSpec as P

HD = 72


norm_eps = 1e-06


def in_order(pieces, dim):
    shape = list(pieces.shape[1:])
    shape[dim] *= pieces.shape[0]
    return jnp.moveaxis(pieces, 0, dim).reshape(shape)


def sent_to_all(shard, axis):
    copies = jnp.broadcast_to(shard, (lax.axis_size(axis), *shard.shape))
    return lax.all_to_all(copies, axis, split_axis=0, concat_axis=0, tiled=True)


def collect(shard, axis, dim):
    return in_order(sent_to_all(shard, axis), dim)


def taken_together(shard, axis):
    return sent_to_all(shard, axis).sum(axis=0)


def in_one(arrays, axis):
    vector, at, outs = (jnp.concatenate([a.reshape(-1) for a in arrays]), 0, [])
    running = taken_together(vector, axis)
    for a in arrays:
        outs.append(running[at : at + a.size].reshape(a.shape))
        at += a.size
    return tuple(outs)


def in_blocks(shard, dim, devices):
    shape = shard.shape
    pieces = shard.reshape(*shape[:dim], devices, shape[dim] // devices, *shape[dim + 1 :])
    return jnp.moveaxis(pieces, dim, 0)


def sum_together(arrays, axis, dims):
    devices = lax.axis_size(axis)
    pieces = [in_blocks(a, dim, devices) for a, dim in zip(arrays, dims)]
    lines = jnp.concatenate([b.reshape(devices, -1) for b in pieces], axis=1)
    span = max(16, -(-lines.shape[1] // 1024) * 8)
    lines = jnp.pad(lines, ((0, 0), (0, span * 128 - lines.shape[1]))).reshape(-1, 128)
    vector, at, outs = (lax.psum_scatter(lines, axis, tiled=True).reshape(-1), 0, [])
    for b in pieces:
        part = b[0]
        outs.append(vector[at : at + part.size].reshape(part.shape))
        at += part.size
    return tuple(outs)


def lookup_rows(indices, table_rows):
    one_hot = (
        indices[:, None] == jnp.arange(table_rows.shape[0], dtype=jnp.int32)[None, :]
    ).astype(table_rows.dtype)
    return jnp.dot(one_hot, table_rows, preferred_element_type=jnp.float32)


def attend(qkv_sums, heads_here):
    batch_rows, seq_len = (qkv_sums.shape[0], qkv_sums.shape[1])
    heads_qkv = qkv_sums.astype(jnp.bfloat16).reshape(batch_rows, seq_len, heads_here, 3, HD)
    queries, key_rows, values = (
        heads_qkv[:, :, :, 0],
        heads_qkv[:, :, :, 1],
        heads_qkv[:, :, :, 2],
    )
    scores = jnp.einsum(
        "blhe,bmhe->bhlm", queries, key_rows, preferred_element_type=jnp.float32
    ) * (1.0 / math.sqrt(HD))
    exponent = jnp.exp(scores - jnp.max(scores, axis=-1, keepdims=True))
    attn_prob = exponent / jnp.sum(exponent, axis=-1, keepdims=True)
    prob_low = attn_prob.astype(jnp.bfloat16)
    attn_mixed = jnp.einsum("bhlm,bmhe->blhe", prob_low, values, preferred_element_type=jnp.float32)
    attn_mixed = attn_mixed.astype(jnp.bfloat16).reshape(batch_rows, seq_len, heads_here * HD)
    return (heads_qkv, attn_prob, prob_low, attn_mixed)


def attend_grad(heads_qkv, attn_prob, prob_low, grad_low):
    batch_rows, seq_len = (heads_qkv.shape[0], heads_qkv.shape[1])
    queries, key_rows, values = (
        heads_qkv[:, :, :, 0],
        heads_qkv[:, :, :, 1],
        heads_qkv[:, :, :, 2],
    )
    grad_probs = jnp.einsum("blhe,bmhe->bhlm", grad_low, values, preferred_element_type=jnp.float32)
    row_delta = jnp.sum(attn_prob * grad_probs, axis=-1, keepdims=True)
    grad_scores = (attn_prob * (grad_probs - row_delta) * (1.0 / math.sqrt(HD))).astype(
        jnp.bfloat16
    )
    grad_query = jnp.einsum(
        "bhlm,bmhe->blhe", grad_scores, key_rows, preferred_element_type=jnp.float32
    )
    grad_keys = jnp.einsum(
        "bhlm,blhe->bmhe", grad_scores, queries, preferred_element_type=jnp.float32
    )
    grad_values = jnp.einsum(
        "bhlm,blhe->bmhe", prob_low, grad_low, preferred_element_type=jnp.float32
    )
    grad_qkv_act = jnp.stack([grad_query, grad_keys, grad_values], axis=3).astype(jnp.bfloat16)
    return grad_qkv_act.reshape(batch_rows, seq_len, -1)


def forward(source, embed_act, qkv_weight, out_weight, ada_weight):
    heads_here = out_weight.shape[0] // HD
    modulation = jnp.einsum(
        "bd,kde->bke", embed_act, ada_weight, preferred_element_type=jnp.float32
    )
    wide_mod = collect(modulation, "tensor", 2)
    full_rows = (
        source.astype(jnp.float32) * (1.0 + wide_mod[:, 1][:, None]) + wide_mod[:, 0][:, None]
    ).astype(jnp.bfloat16)
    qkv_sums = jnp.einsum("bld,df->blf", full_rows, qkv_weight, preferred_element_type=jnp.float32)
    heads_qkv, attn_prob, prob_low, attn_mixed = attend(qkv_sums, heads_here)
    partial_value = jnp.einsum(
        "blf,fd->bld", attn_mixed, out_weight, preferred_element_type=jnp.float32
    )
    projected = lax.psum_scatter(
        partial_value.astype(jnp.bfloat16), "tensor", scatter_dimension=2, tiled=True
    ).astype(jnp.float32)
    branch = modulation[:, 2][:, None] * projected
    return (branch, (full_rows, heads_qkv, attn_prob, prob_low, attn_mixed, projected, modulation))


def local(
    noisy,
    labels,
    tsteps,
    guide_index,
    class_table,
    time_table,
    guide_table,
    guide_weights,
    teacher_qkv,
    teacher_out,
    teacher_ada,
    student_qkv,
    student_out,
    student_ada,
):
    samples, seq_len, width_part = noisy.shape
    model_width = width_part * lax.axis_size("tensor")
    batch_size = samples * lax.axis_size("dp")
    signal = noisy.astype(jnp.float32)
    row_sums = in_one((jnp.sum(signal, axis=2), jnp.sum(signal * signal, axis=2)), "tensor")
    row_mean = row_sums[0] / model_width
    row_var = row_sums[1] / model_width - row_mean * row_mean
    normed = ((signal - row_mean[:, :, None]) * lax.rsqrt(row_var + norm_eps)[:, :, None]).astype(
        jnp.bfloat16
    )
    null_class = class_table.shape[0] - 1
    time_embed = lookup_rows(tsteps, time_table)
    cond_embed = lookup_rows(labels, class_table) + time_embed
    null_embed = class_table[null_class].astype(jnp.float32)[None, :] + time_embed
    guide_hot = guide_index[:, None] == jnp.arange(guide_table.shape[0], dtype=jnp.int32)[None, :]
    student_embed = cond_embed + jnp.dot(
        guide_hot.astype(jnp.bfloat16), guide_table, preferred_element_type=jnp.float32
    )
    strength = jnp.sum(jnp.where(guide_hot, guide_weights[None, :], 0.0), axis=1)
    cond_act = jax.nn.silu(cond_embed).astype(jnp.bfloat16)
    null_act = jax.nn.silu(null_embed).astype(jnp.bfloat16)
    student_act = jax.nn.silu(student_embed).astype(jnp.bfloat16)
    scale_norm = 1.0 / math.sqrt(batch_size * seq_len)
    wide_rows = lax.all_gather(normed, "tensor", axis=2, tiled=True)
    teacher_full = jnp.concatenate([wide_rows, wide_rows], axis=0)
    teacher_act = jnp.concatenate([cond_act, null_act], axis=0)
    teacher_branch, unused_saved = forward(
        teacher_full, teacher_act, teacher_qkv, teacher_out, teacher_ada
    )
    teacher_update = teacher_branch.astype(jnp.bfloat16).astype(jnp.float32)
    scaled = strength[:, None, None]
    target = signal + (
        (1.0 + scaled) * teacher_update[:samples] - scaled * teacher_update[samples:]
    )
    branch, saved = forward(wide_rows, student_act, student_qkv, student_out, student_ada)
    full_rows, heads_qkv, attn_prob, prob_low, attn_mixed, projected, modulation = saved
    heads_here = student_out.shape[0] // HD
    cotangent = (signal + branch - target) * scale_norm
    grad_gate = jnp.sum(cotangent * projected, axis=1)
    grad_proj = (cotangent * modulation[:, 2][:, None]).astype(jnp.bfloat16)
    gathered = lax.all_gather(grad_proj, "tensor", axis=2, tiled=True)
    grad_mixed = jnp.einsum(
        "bld,ed->ble", gathered, student_out, preferred_element_type=jnp.float32
    )
    block_grad = jnp.einsum("ble,bld->ed", attn_mixed, gathered, preferred_element_type=jnp.float32)
    grad_mixed, grad_out_rows = (grad_mixed, block_grad)
    grad_low = grad_mixed.astype(jnp.bfloat16).reshape(samples, seq_len, heads_here, HD)
    grad_qkv_act = attend_grad(heads_qkv, attn_prob, prob_low, grad_low)
    grad_qkv_local = jnp.einsum(
        "bld,blf->df", full_rows, grad_qkv_act, preferred_element_type=jnp.float32
    )
    input_terms = jnp.einsum(
        "blf,df->bld", grad_qkv_act, student_qkv, preferred_element_type=jnp.float32
    )
    grad_input = lax.psum_scatter(
        input_terms.astype(jnp.bfloat16), "tensor", scatter_dimension=2, tiled=True
    ).astype(jnp.float32)
    grad_shift = jnp.sum(grad_input, axis=1)
    grad_scale = jnp.sum(grad_input * normed.astype(jnp.float32), axis=1)
    grad_modulation = jnp.stack([grad_shift, grad_scale, grad_gate], axis=1)
    grad_ada_local = jnp.einsum("bd,bke->kde", student_act.astype(jnp.float32), grad_modulation)
    grad_qkv, grad_out, grad_ada = tuple(
        (
            part.astype(jnp.float32)
            for part in sum_together(
                (
                    grad_qkv_local.astype(jnp.bfloat16),
                    grad_out_rows.astype(jnp.bfloat16),
                    grad_ada_local.astype(jnp.bfloat16),
                ),
                "dp",
                (0, 1, 1),
            )
        )
    )
    return (grad_qkv, grad_out, grad_ada)


def solution(mesh):
    return jax.shard_map(
        local,
        mesh=mesh,
        in_specs=(
            P("dp", None, "tensor"),
            P("dp"),
            P("dp"),
            P("dp"),
            P(),
            P(),
            P(),
            P(),
            P(None, "tensor"),
            P("tensor", None),
            P(None, None, "tensor"),
            P(None, "tensor"),
            P("tensor", None),
            P(None, None, "tensor"),
        ),
        out_specs=(P("dp", "tensor"), P("tensor", "dp"), P(None, "dp", "tensor")),
        check_vma=False,
    )
```

profile of v0, /device:TPU:1, one launch (start us, length us, event | category | flops | bytes accessed | tf_op | source)
XLA Modules:
  0.0 491.4 jit_solution(3670786287526547354)
XLA Ops:
  7.2 1.2 convert_reduce_fusion
  8.7 14.3 %all_to_all.16 = f32[16,1,4096]{2,1,0:T(1,128)S(1)} all-to-all(f32[16,1,4096]{2,1,0:T(1,128)S(1)} %broadcast_in_dim.14), channel_id=1, replica_groups=mesh['dp'=8,'tensor'=16] {'tensor'}, dimensions={0} | all-to-all | bytes 524288 | tf_op jit(solution)/shard_map/all_to_all | solution.py:22
  23.3 1.7 fusion.60
  25.1 0.9 convert_reduce_fusion.2
  27.8 9.7 %all_to_all.17 = f32[16,8,3,72]{3,1,2,0:T(8,128)S(1)} all-to-all(f32[16,8,3,72]{3,1,2,0:T(8,128)S(1)} %broadcast_in_dim.19), channel_id=1, replica_groups=mesh['dp'=8,'tensor'=16] {'tensor'}, dimensions={0} | all-to-all | bytes 221184 | tf_op jit(solution)/shard_map/all_to_all | solution.py:22
  37.6 25.7 %all-gather.3.cloned.1.call-done = bf16[8,256,1152]{1,2,0:T(8,128)(2,1)} async-done(((bf16[8,256,72]{1,2,0:T(8,128)(2,1)}), bf16[8,256,1152]{1,2,0:T(8,128)(2,1)}) %all-gather.3.cloned.1.call-update) | async-done | bytes 4718608 | tf_op jit(solution)/shard_map/all_gather | solution.py:173
  63.3 5.4 %fusion.34 = bf16[8,256,216]{1,2,0:T(8,128)(2,1)S(1)} fusion(bf16[8,256,1152]{1,2,0:T(8,128)(2,1)} %all-gather.3.cloned.1.call-done, f32[8,1152]{1,0:T(8,128)S(1)} %get-tuple-element.14, f32[8,1152]{1,0:T(8,128)S(1)} %get-tuple-element.13, bf16[1152,216]{0,1:T(8,128)(2,1)S(1)} %copy-done.5), kind=kOutput, calls=%fused_computation.43 | convolution fusion | flops 1029095424 | bytes 6174720 | tf_op jit(solution)/shard_map/bld,df->blf/dot_general | solution.py:122
  68.8 2.3 fusion.101
  71.0 2.0 fusion.49
  73.0 1.4 fusion.105
  74.4 2.9 copy.153
  77.4 1.0 copy-done.7
  78.7 13.0 %all_to_all.18 = f32[16,16,3,72]{3,1,2,0:T(8,128)S(1)} all-to-all(f32[16,16,3,72]{3,1,2,0:T(8,128)S(1)} %broadcast_in_dim.22), channel_id=1, replica_groups=mesh['dp'=8,'tensor'=16] {'tensor'}, dimensions={0} | all-to-all | bytes 442368 | tf_op jit(solution)/shard_map/all_to_all | solution.py:22
  92.0 9.6 %fusion.27 = bf16[16,256,216]{1,2,0:T(8,128)(2,1)S(1)} fusion(bf16[8,256,1152]{1,2,0:T(8,128)(2,1)} %all-gather.3.cloned.1.call-done, f32[16,1152]{1,0:T(8,128)S(1)} %get-tuple-element.12, f32[16,1152]{1,0:T(8,128)S(1)} %get-tuple-element.11, bf16[1152,216]{0,1:T(8,128)(2,1)} %param.22), kind=kOutput, calls=%fused_computation.40 | convolution fusion | flops 2062909440 | bytes 7133184 | tf_op jit(solution)/shard_map/bld,df->blf/dot_general | solution.py:122
  101.6 0.8 fusion.64
  102.4 3.0 fusion.100
  105.4 8.2 %fusion.102 = bf16[144,8,16,256]{3,1,0,2:T(8,128)(2,1)} fusion(bf16[72,1152]{1,0:T(8,128)(2,1)S(1)} %copy-done.11, f32[16,256,256]{1,2,0:T(8,128)} %get-tuple-element.22, f32[16,256]{1,0:T(8,128)S(1)} %get-tuple-element.21, bf16[16,256,1,3,72]{1,4,3,0,2:T(8,128)(2,1)S(1)} %bitcast.225), kind=kOutput, calls=%fused_computation.151 | convolution fusion | flops 837582848 | bytes 14403584 | tf_op jit(solution)/shard_map/blf,fd->bld/dot_general | solution.py:124
  113.6 8.7 %copy.155 = bf16[144,8,16,256]{3,1,2,0:T(8,128)(2,1)} copy(bf16[144,8,16,256]{3,1,0,2:T(8,128)(2,1)} %fusion.102) | data formatting | bytes 18874368
  123.1 25.3 %reduce-scatter.10.cloned.1.call-done = bf16[72,2048]{1,0:T(8,128)(2,1)} async-done(((bf16[1152,2048]{1,0:T(8,128)(2,1)}), bf16[72,2048]{1,0:T(8,128)(2,1)}) %reduce-scatter.10.cloned.1.call-update) | async-done | bytes 294928
  148.4 1.0 copy.154
  149.5 108.1 %reduce-scatter.12.cloned.1.call-done = bf16[72,4096]{1,0:T(8,128)(2,1)} async-done(((bf16[1152,4096]{1,0:T(8,128)(2,1)}), bf16[72,4096]{1,0:T(8,128)(2,1)}) %reduce-scatter.12.cloned.1.call-update) | async-done | bytes 589840
  257.5 1.2 copy.156
  259.0 1.1 multiply_convert_fusion.2
  260.1 40.1 %all-gather.5.cloned.1.call-done = bf16[8,256,1152]{1,2,0:T(8,128)(2,1)} async-done(((bf16[8,256,72]{1,2,0:T(8,128)(2,1)}), bf16[8,256,1152]{1,2,0:T(8,128)(2,1)}) %all-gather.5.cloned.1.call-update) | async-done | bytes 4718608 | tf_op jit(solution)/shard_map/all_gather | solution.py:190
  300.3 3.4 convolution_convert_fusion.4
  304.1 2.8 fusion.71
  307.0 4.5 fusion.43
  311.5 4.4 fusion.46
  316.1 1.4 fusion.108
  317.5 2.8 copy.157
  320.6 3.9 fusion.20
  325.0 0.9 reshape.230
  325.9 5.3 %fusion.15 = bf16[1152,216]{0,1:T(8,128)(2,1)S(1)} fusion(bf16[8,256,216]{1,2,0:T(8,128)(2,1)S(1)} %bitcast.215, bf16[8,256,1152]{1,2,0:T(8,128)(2,1)} %all-gather.3.cloned.1.call-done, f32[8,1152]{1,0:T(8,128)S(1)} %get-tuple-element.14, f32[8,1152]{1,0:T(8,128)S(1)} %get-tuple-element.13), kind=kOutput, calls=%fused_computation.22 | convolution fusion | flops 1028901888 | bytes 6174720 | tf_op jit(solution)/shard_map/bld,blf->df/dot_general | solution.py:198
  331.4 1.7 reshape_reshape.3
  333.1 53.9 %reduce-scatter.14.cloned.1.call-done = bf16[72,2048]{1,0:T(8,128)(2,1)} async-done(((bf16[1152,2048]{1,0:T(8,128)(2,1)}), bf16[72,2048]{1,0:T(8,128)(2,1)}) %reduce-scatter.14.cloned.1.call-update) | async-done | bytes 294928
  387.0 1.0 copy.158
  388.7 1.1 reshape.231
  389.9 1.4 copy.127
  391.3 1.8 reshape.232
  393.2 1.5 fusion.52
  394.7 1.6 reshape.233
  396.3 0.6 dynamic-slice
  397.5 82.9 %all-reduce.4.cloned.1.call-done = bf16[4544,128]{1,0:T(8,128)(2,1)} async-done(((bf16[4544,128]{1,0:T(8,128)(2,1)}), bf16[4544,128]{1,0:T(8,128)(2,1)}) %all-reduce.4.cloned.1.call-update) | async-done | bytes 1163280
  480.4 0.9 dynamic-slice_convert_fusion
  481.3 0.9 reshape.235
  482.2 0.7 dynamic-slice_convert_fusion.2
  482.9 0.7 reshape.236
  483.6 0.9 reshape.237
  (82 shorter events, 6.7 us)
Async XLA Ops:
  7.2 18.8 %copy-start = (bf16[1000,1152]{1,0:T(8,128)(2,1)S(1)}, bf16[1000,1152]{1,0:T(8,128)(2,1)}, u32[]{:S(2)}) copy-start(bf16[1000,1152]{1,0:T(8,128)(2,1)} %param.19) | copy-start | bytes 6912004
  7.2 18.8 %copy-start.10 = (s32[8]{0:T(128)S(1)}, s32[8]{0:T(128)}, u32[]{:S(2)}) copy-start(s32[8]{0:T(128)} %param.16) | copy-start | bytes 100
  7.2 56.1 %all-gather.3.cloned.1.call-start = ((), (), s32[]{:S(2)}) async-start(), calls=%async_computation.6 | async-start | bytes 5013504 | tf_op jit(solution)/shard_map/all_gather | solution.py:173
  8.5 18.0 %copy-start.9 = (s32[8]{0:T(128)S(1)}, s32[8]{0:T(128)}, u32[]{:S(2)}) copy-start(s32[8]{0:T(128)} %param.15) | copy-start | bytes 100
  25.0 123.4 %reduce-scatter.10.cloned.1.call-start = ((), (), s32[]{:S(2)}) async-start(), calls=%async_computation.8 | async-start | bytes 5013504
  25.1 1.7 copy-start.3
  26.0 1.2 copy-start.12
  26.0 1.2 copy-start.13
  26.0 1.4 copy-start.6
  26.8 36.6 %copy-start.5 = (bf16[1152,216]{0,1:T(8,128)(2,1)S(1)}, bf16[1152,216]{0,1:T(8,128)(2,1)}, u32[]{:S(2)}) copy-start(bf16[1152,216]{0,1:T(8,128)(2,1)} %param.25) | copy-start | bytes 1492996
  68.8 4.2 copy-start.8
  71.0 2.0 copy-start.4
  77.4 1.0 copy-start.7
  77.4 180.2 %reduce-scatter.12.cloned.1.call-start = ((), (), s32[]{:S(2)}) async-start(), calls=%async_computation.9 | async-start | bytes 10027008
  102.4 3.0 copy-start.11
  122.3 0.7 copy-start.14
  122.3 136.7 %copy-start.2 = (bf16[8,256,72]{1,2,0:T(8,128)(2,1)S(1)}, bf16[8,256,72]{1,2,0:T(8,128)(2,1)}, u32[]{:S(2)}) copy-start(bf16[8,256,72]{1,2,0:T(8,128)(2,1)} %param.14) | copy-start | bytes 884740
  122.3 177.9 %all-gather.5.cloned.1.call-start = ((), (), s32[]{:S(2)}) async-start(), calls=%async_computation.7 | async-start | bytes 5013504 | tf_op jit(solution)/shard_map/all_gather | solution.py:190
  260.1 126.9 %reduce-scatter.14.cloned.1.call-start = ((), (), s32[]{:S(2)}) async-start(), calls=%async_computation.10 | async-start | bytes 5013504
  300.3 3.4 copy-start.16
  320.4 160.0 %all-reduce.4.cloned.1.call-start = ((), (), s32[]{:S(2)}) async-start(), calls=%async_computation.11 | async-start | bytes 2326528
  393.2 91.4 %copy-start.1 = (bf16[1000,1152]{1,0:T(8,128)(2,1)S(1)}, bf16[1000,1152]{1,0:T(8,128)(2,1)}, u32[]{:S(2)}) copy-start(bf16[1000,1152]{1,0:T(8,128)(2,1)} %param.19) | copy-start | bytes 6912004
  394.7 1.6 copy-start.15
Sparse Core Ops, SparseCore 0:
  25.1 38.1 all-gather.2
  77.5 70.8 reduce-scatter.9
  150.9 106.6 reduce-scatter.11
  260.2 39.9 all-gather.4
  320.5 66.4 reduce-scatter.13
  396.4 83.9 all-reduce.3
where the time goes:
time: 497 us; the launch traced here: 491 us
  waiting for transfers between devices  336 us (68%)
  matrix products  57.8 us (12%)
  blocking collectives  37 us (7%)
  local copies, waits for them, and re-layouts  32.6 us (7%)
  between operations  15.2 us (3%)
  other arithmetic  12.4 us (2%)
    unnamed x10, waiting for transfers between devices  270 us
    all_gather x1, waiting for transfers between devices, local(): gathered = lax.all_gather(grad_proj, 'tensor', axis=2, tiled=True)  40.1 us
    all_to_all x3, blocking collectives, sent_to_all(): return lax.all_to_all(copies, axis, split_axis=0, concat_axis=0, tiled=True)  37 us
    all_gather x1, waiting for transfers between devices, local(): wide_rows = lax.all_gather(normed, 'tensor', axis=2, tiled=True)  25.7 us
    unnamed x43, local copies, waits for them, and re-layouts  19.9 us
    dot_general x2, matrix products, forward(): jnp.einsum('bld,df->blf', full_rows, qkv_weight, preferred_element_type=j...  15 us
  transfers between devices with their start and end apart: 6, of which 6 were waited for; matrix products, arithmetic and copies ran while one was open for 10% of the time, Pallas kernels for 0%

commit v1 on v0

--- a/solution.py
+++ b/solution.py
@@ -110,25 +110,12 @@
     return grad_qkv_act.reshape(batch_rows, seq_len, -1)
 
 
-def forward(source, embed_act, qkv_weight, out_weight, ada_weight):
-    heads_here = out_weight.shape[0] // HD
-    modulation = jnp.einsum(
-        "bd,kde->bke", embed_act, ada_weight, preferred_element_type=jnp.float32
-    )
-    wide_mod = collect(modulation, "tensor", 2)
+def forward(normed, wide_mod, qkv_weight, heads_here):
     full_rows = (
-        source.astype(jnp.float32) * (1.0 + wide_mod[:, 1][:, None]) + wide_mod[:, 0][:, None]
+        normed.astype(jnp.float32) * (1.0 + wide_mod[:, 1][:, None]) + wide_mod[:, 0][:, None]
     ).astype(jnp.bfloat16)
     qkv_sums = jnp.einsum("bld,df->blf", full_rows, qkv_weight, preferred_element_type=jnp.float32)
-    heads_qkv, attn_prob, prob_low, attn_mixed = attend(qkv_sums, heads_here)
-    partial_value = jnp.einsum(
-        "blf,fd->bld", attn_mixed, out_weight, preferred_element_type=jnp.float32
-    )
-    projected = lax.psum_scatter(
-        partial_value.astype(jnp.bfloat16), "tensor", scatter_dimension=2, tiled=True
-    ).astype(jnp.float32)
-    branch = modulation[:, 2][:, None] * projected
-    return (branch, (full_rows, heads_qkv, attn_prob, prob_low, attn_mixed, projected, modulation))
+    return attend(qkv_sums, heads_here)
 
 
 def local(
@@ -149,14 +136,10 @@
 ):
     samples, seq_len, width_part = noisy.shape
     model_width = width_part * lax.axis_size("tensor")
-    batch_size = samples * lax.axis_size("dp")
-    signal = noisy.astype(jnp.float32)
-    row_sums = in_one((jnp.sum(signal, axis=2), jnp.sum(signal * signal, axis=2)), "tensor")
-    row_mean = row_sums[0] / model_width
-    row_var = row_sums[1] / model_width - row_mean * row_mean
-    normed = ((signal - row_mean[:, :, None]) * lax.rsqrt(row_var + norm_eps)[:, :, None]).astype(
-        jnp.bfloat16
-    )
+    dp = lax.axis_size("dp")
+    batch_size = samples * dp
+    heads_here = student_out.shape[0] // HD
+    wide = lax.all_gather(noisy, "tensor", axis=2, tiled=True)
     null_class = class_table.shape[0] - 1
     time_embed = lookup_rows(tsteps, time_table)
     cond_embed = lookup_rows(labels, class_table) + time_embed
@@ -169,59 +152,82 @@
     cond_act = jax.nn.silu(cond_embed).astype(jnp.bfloat16)
     null_act = jax.nn.silu(null_embed).astype(jnp.bfloat16)
     student_act = jax.nn.silu(student_embed).astype(jnp.bfloat16)
+    teacher_act = jnp.concatenate([cond_act, null_act], axis=0)
+    mod_t = jnp.einsum("bd,kde->bke", teacher_act, teacher_ada, preferred_element_type=jnp.float32)
+    mod_s = jnp.einsum("bd,kde->bke", student_act, student_ada, preferred_element_type=jnp.float32)
+    wide_mod = collect(jnp.concatenate([mod_t, mod_s], axis=0), "tensor", 2)
+    cond_mod, null_mod, student_mod = (
+        wide_mod[:samples],
+        wide_mod[samples : 2 * samples],
+        wide_mod[2 * samples :],
+    )
     scale_norm = 1.0 / math.sqrt(batch_size * seq_len)
-    wide_rows = lax.all_gather(normed, "tensor", axis=2, tiled=True)
-    teacher_full = jnp.concatenate([wide_rows, wide_rows], axis=0)
-    teacher_act = jnp.concatenate([cond_act, null_act], axis=0)
-    teacher_branch, unused_saved = forward(
-        teacher_full, teacher_act, teacher_qkv, teacher_out, teacher_ada
-    )
-    teacher_update = teacher_branch.astype(jnp.bfloat16).astype(jnp.float32)
-    scaled = strength[:, None, None]
-    target = signal + (
-        (1.0 + scaled) * teacher_update[:samples] - scaled * teacher_update[samples:]
-    )
-    branch, saved = forward(wide_rows, student_act, student_qkv, student_out, student_ada)
-    full_rows, heads_qkv, attn_prob, prob_low, attn_mixed, projected, modulation = saved
-    heads_here = student_out.shape[0] // HD
-    cotangent = (signal + branch - target) * scale_norm
-    grad_gate = jnp.sum(cotangent * projected, axis=1)
-    grad_proj = (cotangent * modulation[:, 2][:, None]).astype(jnp.bfloat16)
-    gathered = lax.all_gather(grad_proj, "tensor", axis=2, tiled=True)
+    signal = wide.astype(jnp.float32)
+    row_mean = jnp.sum(signal, axis=2) / model_width
+    row_var = jnp.sum(signal * signal, axis=2) / model_width - row_mean * row_mean
+    normed = ((signal - row_mean[:, :, None]) * lax.rsqrt(row_var + norm_eps)[:, :, None]).astype(
+        jnp.bfloat16
+    )
+    teacher_mixed = forward(
+        jnp.concatenate([normed, normed], axis=0), wide_mod[: 2 * samples], teacher_qkv, heads_here
+    )[3]
+    heads_qkv, attn_prob, prob_low, attn_mixed = forward(
+        normed, student_mod, student_qkv, heads_here
+    )
+    teacher_part = jnp.einsum(
+        "blf,fd->bld", teacher_mixed, teacher_out, preferred_element_type=jnp.float32
+    )
+    student_part = jnp.einsum(
+        "blf,fd->bld", attn_mixed, student_out, preferred_element_type=jnp.float32
+    )
+    gate = student_mod[:, 2] * scale_norm
+    cond_gate = (1.0 + strength)[:, None] * cond_mod[:, 2] * scale_norm
+    null_gate = strength[:, None] * null_mod[:, 2] * scale_norm
+    partial_cot = (
+        gate[:, None] * student_part
+        - cond_gate[:, None] * teacher_part[:samples]
+        + null_gate[:, None] * teacher_part[samples:]
+    )
+    piece = lax.psum_scatter(
+        partial_cot.astype(jnp.bfloat16), "tensor", scatter_dimension=2, tiled=True
+    )
+    cotangent = lax.all_gather(piece, "tensor", axis=2, tiled=True)
+    grad_proj = (cotangent.astype(jnp.float32) * student_mod[:, 2][:, None]).astype(jnp.bfloat16)
     grad_mixed = jnp.einsum(
-        "bld,ed->ble", gathered, student_out, preferred_element_type=jnp.float32
-    )
-    block_grad = jnp.einsum("ble,bld->ed", attn_mixed, gathered, preferred_element_type=jnp.float32)
-    grad_mixed, grad_out_rows = (grad_mixed, block_grad)
+        "bld,ed->ble", grad_proj, student_out, preferred_element_type=jnp.float32
+    )
+    image_out = jnp.einsum("ble,bld->bed", attn_mixed, cotangent, preferred_element_type=jnp.float32)
+    grad_out_rows = jnp.sum(image_out * student_mod[:, 2][:, None], axis=0)
+    grad_gate = jnp.sum(image_out * student_out.astype(jnp.float32)[None], axis=1)
     grad_low = grad_mixed.astype(jnp.bfloat16).reshape(samples, seq_len, heads_here, HD)
     grad_qkv_act = attend_grad(heads_qkv, attn_prob, prob_low, grad_low)
-    grad_qkv_local = jnp.einsum(
-        "bld,blf->df", full_rows, grad_qkv_act, preferred_element_type=jnp.float32
-    )
-    input_terms = jnp.einsum(
-        "blf,df->bld", grad_qkv_act, student_qkv, preferred_element_type=jnp.float32
-    )
-    grad_input = lax.psum_scatter(
-        input_terms.astype(jnp.bfloat16), "tensor", scatter_dimension=2, tiled=True
+    image_qkv = jnp.einsum("bld,blf->bdf", normed, grad_qkv_act, preferred_element_type=jnp.float32)
+    column_sums = jnp.sum(grad_qkv_act.astype(jnp.float32), axis=1)
+    grad_qkv_local = jnp.sum(
+        image_qkv * (1.0 + student_mod[:, 1])[:, :, None]
+        + student_mod[:, 0][:, :, None] * column_sums[:, None, :],
+        axis=0,
+    )
+    weight = student_qkv.astype(jnp.float32)
+    grad_scale = jnp.sum(image_qkv * weight[None], axis=2)
+    grad_shift = jnp.einsum("bf,df->bd", column_sums, weight, precision=lax.Precision.HIGHEST)
+    grad_modulation = lax.psum_scatter(
+        jnp.stack([grad_shift, grad_scale, grad_gate], axis=1),
+        "tensor",
+        scatter_dimension=2,
+        tiled=True,
+    )
+    all_mod = lax.all_gather(grad_modulation, "dp", axis=0, tiled=True)
+    act_rows = lax.all_to_all(student_act, "dp", split_axis=1, concat_axis=0, tiled=True)
+    grad_ada = jnp.einsum(
+        "bd,bke->kde", act_rows.astype(jnp.float32), all_mod, precision=lax.Precision.HIGHEST
+    )
+    grad_qkv = lax.psum_scatter(
+        grad_qkv_local.astype(jnp.bfloat16), "dp", scatter_dimension=0, tiled=True
     ).astype(jnp.float32)
-    grad_shift = jnp.sum(grad_input, axis=1)
-    grad_scale = jnp.sum(grad_input * normed.astype(jnp.float32), axis=1)
-    grad_modulation = jnp.stack([grad_shift, grad_scale, grad_gate], axis=1)
-    grad_ada_local = jnp.einsum("bd,bke->kde", student_act.astype(jnp.float32), grad_modulation)
-    grad_qkv, grad_out, grad_ada = tuple(
-        (
-            part.astype(jnp.float32)
-            for part in sum_together(
-                (
-                    grad_qkv_local.astype(jnp.bfloat16),
-                    grad_out_rows.astype(jnp.bfloat16),
-                    grad_ada_local.astype(jnp.bfloat16),
-                ),
-                "dp",
-                (0, 1, 1),
-            )
-        )
-    )
+    grad_out = lax.psum_scatter(
+        grad_out_rows.astype(jnp.bfloat16), "dp", scatter_dimension=1, tiled=True
+    ).astype(jnp.float32)
     return (grad_qkv, grad_out, grad_ada)
 
 

time: 497 us -> 512 us (1.030)
  waiting for transfers between devices: 336 us -> 355 us
  local copies, waits for them, and re-layouts: 32.6 us -> 14.4 us
  starting transfers between devices: 0.43 us -> 14.2 us
  matrix products: 57.8 us -> 71.5 us
  blocking collectives: 37 us -> 28.4 us
    all_to_all x3 -> x0, blocking collectives: 37 us -> none  [sent_to_all(): return lax.all_to_all(copies, axis, split_axis=0, concat_axis=0, tiled=True)]
    all_gather x0 -> x1, blocking collectives: none -> 28.4 us  [local(): all_mod = lax.all_gather(grad_modulation, 'dp', axis=0, tiled=True)]
    all_to_all x0 -> x2, waiting for transfers between devices: none -> 15.1 us  [the longest x1 15.1 us: sent_to_all(): return lax.all_to_all(copies, axis, split_axis=0, concat_axis=0, tiled=True)]
    all_to_all x0 -> x2, starting transfers between devices: none -> 13.7 us  [the longest x1 7.16 us: sent_to_all(): return lax.all_to_all(copies, axis, split_axis=0, concat_axis=0, tiled=True)]
    unnamed x10, waiting for transfers between devices: 270 us -> 282 us
    dot_general x9, matrix products: 24.4 us -> 36 us  [the longest x1 11.7 us: local(): jnp.einsum('blf,fd->bld', teacher_mixed, teacher_out, preferred_element_t...]
    unnamed x43 -> x51, local copies, waits for them, and re-layouts: 19.9 us -> 11.8 us
    reshape x9 -> x0, local copies, waits for them, and re-layouts: 7.7 us -> none  [the longest x4 3.03 us: in_blocks(): shard.reshape(*shape[:dim], devices, shape[dim] // devices, *shape[dim +...]
  transfers between devices with their start and end apart: 6 -> 8, of which waited for: 6 -> 7; matrix products, arithmetic and copies ran while one was open for 10% -> 3% of each run, Pallas kernels for 0% -> 0%
where the time goes in v1:
time: 512 us; the launch traced here: 510 us
  waiting for transfers between devices  355 us (69%)
  matrix products  71.5 us (14%)
  blocking collectives  28.4 us (6%)
  between operations  15.2 us (3%)
  local copies, waits for them, and re-layouts  14.4 us (3%)
  starting transfers between devices  14.2 us (3%)
  other arithmetic  11.2 us (2%)
    unnamed x10, waiting for transfers between devices  282 us
    all_gather x1, waiting for transfers between devices, local(): cotangent = lax.all_gather(piece, 'tensor', axis=2, tiled=True)  38.9 us
    all_gather x1, blocking collectives, local(): all_mod = lax.all_gather(grad_modulation, 'dp', axis=0, tiled=True)  28.4 us
    all_gather x1, waiting for transfers between devices, local(): wide = lax.all_gather(noisy, 'tensor', axis=2, tiled=True)  19.2 us
    all_to_all x1, waiting for transfers between devices, sent_to_all(): return lax.all_to_all(copies, axis, split_axis=0, concat_axis=0, tiled=True)  15.1 us
    dot_general x2, matrix products, forward(): jnp.einsum('bld,df->blf', full_rows, qkv_weight, preferred_element_type=j...  14.9 us
    unnamed x51, local copies, waits for them, and re-layouts  11.8 us
    dot_general x1, matrix products, local(): jnp.einsum('blf,fd->bld', teacher_mixed, teacher_out, preferred_element_t...  11.7 us
  transfers between devices with their start and end apart: 8, of which 7 were waited for; matrix products, arithmetic and copies ran while one was open for 3% of the time, Pallas kernels for 0%

profile of v1, /device:TPU:1, one launch (start us, length us, event | category | flops | bytes accessed | tf_op | source)
XLA Modules:
  0.0 510.3 jit_solution(7823777829901788523)
XLA Ops:
  7.3 0.7 all-gather.3.cloned.1.call-update
  8.0 1.0 convert_reduce_fusion.2
  9.0 1.1 multiply_convert_fusion.6
  10.1 2.2 multiply_convert_fusion.7
  13.1 0.9 broadcast_in_dim.10
  14.0 7.2 %all-to-all-start = ((f32[16,24,3,72]{3,1,2,0:T(8,128)}), f32[16,24,3,72]{3,1,2,0:T(8,128)S(1)}, u32[]{:S(2)}, u32[]{:S(2)}) async-start(f32[16,24,3,72]{3,1,2,0:T(8,128)} %broadcast_in_dim.10), calls=%async_computation | async-start | bytes 1179648 | tf_op jit(solution)/shard_map/all_to_all | solution.py:22
  21.4 15.1 %all-to-all-done = f32[16,24,3,72]{3,1,2,0:T(8,128)S(1)} async-done(((f32[16,24,3,72]{3,1,2,0:T(8,128)}), f32[16,24,3,72]{3,1,2,0:T(8,128)S(1)}, u32[]{:S(2)}, u32[]{:S(2)}) %all-to-all-start) | async-done | bytes 331808 | tf_op jit(solution)/shard_map/all_to_all | solution.py:22
  37.6 19.2 %all-gather.3.cloned.1.call-done = bf16[8,256,1152]{1,2,0:T(8,128)(2,1)} async-done(((bf16[8,256,72]{1,2,0:T(8,128)(2,1)}), bf16[8,256,1152]{1,2,0:T(8,128)(2,1)}) %all-gather.3.cloned.1.call-update) | async-done | bytes 4718608 | tf_op jit(solution)/shard_map/all_gather | solution.py:142
  56.8 3.7 convert_reduce_fusion
  60.6 1.1 fusion.4
  61.7 9.5 %fusion.29 = bf16[16,256,216]{1,2,0:T(8,128)(2,1)S(1)} fusion(bf16[8,256,1152]{1,2,0:T(8,128)(2,1)S(1)} %fusion.4, f32[16,1152]{1,0:T(8,128)S(1)} %get-tuple-element.33, f32[16,1152]{1,0:T(8,128)S(1)} %get-tuple-element.32, bf16[1152,216]{0,1:T(8,128)(2,1)S(1)} %copy-done.11), kind=kOutput, calls=%fused_computation.49 | convolution fusion | flops 2062909440 | bytes 7133184 | tf_op jit(solution)/shard_map/bld,df->blf/dot_general | solution.py:117
  71.2 0.8 fusion.51
  72.0 1.1 fusion.97
  73.4 5.4 %fusion.36 = bf16[8,256,216]{1,2,0:T(8,128)(2,1)} fusion(bf16[8,256,1152]{1,2,0:T(8,128)(2,1)S(1)} %fusion.4, f32[8,1152]{1,0:T(8,128)S(1)} %get-tuple-element.36, f32[8,1152]{1,0:T(8,128)S(1)} %get-tuple-element.37, bf16[1152,216]{0,1:T(8,128)(2,1)S(1)} %copy-done.5), kind=kOutput, calls=%fused_computation.52 | convolution fusion | flops 1029095424 | bytes 6174720 | tf_op jit(solution)/shard_map/bld,df->blf/dot_general | solution.py:117
  78.8 3.3 fusion.98
  82.0 11.7 %fusion.39 = f32[16,256,1152]{1,2,0:T(8,128)} fusion(f32[16,256]{1,0:T(8,128)S(1)} %fusion.97, bf16[16,256,1,3,72]{1,4,3,0,2:T(8,128)(2,1)S(1)} %bitcast.190, f32[16,256,256]{1,2,0:T(8,128)} %copy-done.4, bf16[72,1152]{1,0:T(8,128)(2,1)S(1)} %copy-done.8), kind=kOutput, calls=%fused_computation.55 | convolution fusion | flops 836014336 | bytes 28035072 | tf_op jit(solution)/shard_map/blf,fd->bld/dot_general | solution.py:177
  93.8 2.1 fusion.47
  95.8 11.0 %fusion.99 = bf16[144,8,8,256]{3,1,0,2:T(8,128)(2,1)S(1)} fusion(f32[16,256,1152]{1,2,0:T(8,128)} %fusion.39, f32[8,1152]{1,0:T(8,128)S(1)} %fusion.69, f32[8,1152]{1,0:T(8,128)S(1)} %get-tuple-element.46, bf16[8,256,72]{1,2,0:T(8,128)(2,1)S(1)} %fusion.47, bf16[72,1152]{1,0:T(8,128)(2,1)S(1)} %copy-done.9, f32[8,1152]{1,0:T(8,128)S(1)} %get-tuple-element.35), kind=kOutput, calls=%fused_computation.135 | convolution fusion | flops 353894400 | bytes 24164352 | tf_op jit(solution)/shard_map/blf,fd->bld/dot_general | solution.py:180
  106.8 2.8 copy.180
  109.9 66.2 %reduce-scatter.11.cloned.1.call-done = bf16[72,2048]{1,0:T(8,128)(2,1)} async-done(((bf16[1152,2048]{1,0:T(8,128)(2,1)}), bf16[72,2048]{1,0:T(8,128)(2,1)}) %reduce-scatter.11.cloned.1.call-update) | async-done | bytes 294928
  176.1 1.0 copy.181
  177.1 0.8 copy.167
  178.0 1.0 convert_element_type.156
  179.0 38.9 %all-gather.5.cloned.1.call-done = bf16[8,256,1152]{1,2,0:T(8,128)(2,1)} async-done(((bf16[8,256,72]{1,2,0:T(8,128)(2,1)}), bf16[8,256,1152]{1,2,0:T(8,128)(2,1)}) %all-gather.5.cloned.1.call-update) | async-done | bytes 4718608 | tf_op jit(solution)/shard_map/all_gather | solution.py:194
  217.9 4.3 fusion.46
  222.2 2.1 convolution_bitcast_fusion.1
  224.2 1.5 fusion.63
  225.7 3.8 fusion.43
  229.5 3.8 fusion.40
  233.3 1.5 convert_reduce_fusion.1
  235.3 6.2 %multiply_reduce_fusion = (f32[8,1152]{1,0:T(8,128)S(1)}, bf16[1152,216]{0,1:T(8,128)(2,1)S(1)}) fusion(f32[1152,216]{0,1:T(8,128)} %convert_element_type.156, f32[8,216]{1,0:T(8,128)S(1)} %mul.229, f32[8,1152]{1,0:T(8,128)S(1)} %get-tuple-element.36, f32[8,1152]{1,0:T(8,128)} %copy-done.10, bf16[8,256,1152]{1,2,0:T(8,128)(2,1)} %copy-done.3, ...), kind=kOutput, calls=%fused_computation.23 | convolution fusion | flops 1030901760 | bytes 7213824 | tf_op jit(solution)/shard_map/bld,blf->bdf/dot_general | solution.py:204
  241.6 1.6 multiply_reduce_fusion.2
  243.2 0.7 pad_maximum_fusion
  244.0 0.9 copy.170
  244.9 1.1 copy.168
  246.1 0.6 copy.153
  246.7 6.6 %all-to-all-start.1 = ((bf16[8,8,144]{2,0,1:T(8,128)(2,1)}), bf16[8,8,144]{2,0,1:T(8,128)(2,1)S(1)}, u32[]{:S(2)}, u32[]{:S(2)}) async-start(bf16[8,8,144]{2,0,1:T(8,128)(2,1)} %copy.153), calls=%async_computation.1 | async-start | bytes 65536 | tf_op jit(solution)/shard_map/all_to_all | solution.py:221
  253.3 0.6 dynamic-slice
  254.6 103.1 %all-reduce.3.cloned.1.call-done = f32[8,3,1152]{2,0,1:T(8,128)} async-done(((f32[8,3,1152]{2,0,1:T(8,128)}), f32[8,3,1152]{2,0,1:T(8,128)}) %all-reduce.3.cloned.1.call-update) | async-done | bytes 110608
  357.6 0.8 constant_dynamic-slice_fusion
  358.4 28.4 %all_gather.11 = f32[64,3,72]{2,0,1:T(8,128)S(1)} all-gather(f32[8,3,72]{2,0,1:T(8,128)S(1)} %constant_dynamic-slice_fusion), channel_id=1, replica_groups=mesh['dp'=8,'tensor'=16] {'dp'}, dimensions={0}, use_global_device_ids=true | all-gather | bytes 62208 | tf_op jit(solution)/shard_map/all_gather | solution.py:220
  387.1 0.8 copy.155
  387.9 38.9 %reduce-scatter.15.cloned.1.call-done = bf16[144,72]{1,0:T(8,128)(2,1)} async-done(((bf16[1152,72]{1,0:T(8,128)(2,1)}), bf16[144,72]{1,0:T(8,128)(2,1)}) %reduce-scatter.15.cloned.1.call-update) | async-done | bytes 20752
  426.9 0.8 copy.171
  427.7 0.6 convert_element_type.155
  428.4 73.3 %reduce-scatter.13.cloned.1.call-done = bf16[144,216]{1,0:T(8,128)(2,1)} async-done(((bf16[1152,216]{1,0:T(8,128)(2,1)}), bf16[144,216]{1,0:T(8,128)(2,1)}) %reduce-scatter.13.cloned.1.call-update) | async-done | bytes 62224
  501.7 1.0 copy.169
  502.7 0.8 copy.154
  (80 shorter events, 3.9 us)
Async XLA Ops:
  7.2 1.8 copy-start
  7.2 5.1 copy-start.12
  7.2 5.1 copy-start.13
  7.2 5.3 %copy-start.6 = (bf16[3,1152,72]{1,2,0:T(8,128)(2,1)S(1)}, bf16[3,1152,72]{1,2,0:T(8,128)(2,1)}, u32[]{:S(2)}) copy-start(bf16[3,1152,72]{1,2,0:T(8,128)(2,1)} %param.24) | copy-start | bytes 1492996
  7.2 5.6 %copy-start.7 = (bf16[3,1152,72]{1,2,0:T(8,128)(2,1)S(1)}, bf16[3,1152,72]{1,2,0:T(8,128)(2,1)}, u32[]{:S(2)}) copy-start(bf16[3,1152,72]{1,2,0:T(8,128)(2,1)} %param.27) | copy-start | bytes 1492996
  7.2 14.0 %copy-start.14 = (f32[32]{0:T(128)S(1)}, f32[32]{0:T(128)}, u32[]{:S(2)}) copy-start(f32[32]{0:T(128)} %param.21) | copy-start | bytes 388
  7.2 49.6 %all-gather.3.cloned.1.call-start = ((), (), s32[]{:S(2)}) async-start(), calls=%async_computation.5 | async-start | bytes 5013504 | tf_op jit(solution)/shard_map/all_gather | solution.py:142
  14.0 22.5 %all-to-all-start = ((f32[16,24,3,72]{3,1,2,0:T(8,128)}), f32[16,24,3,72]{3,1,2,0:T(8,128)S(1)}, u32[]{:S(2)}, u32[]{:S(2)}) async-start(f32[16,24,3,72]{3,1,2,0:T(8,128)} %broadcast_in_dim.10), calls=%async_computation | async-start | bytes 1179648 | tf_op jit(solution)/shard_map/all_to_all | solution.py:22
  21.1 154.9 %reduce-scatter.11.cloned.1.call-start = ((), (), s32[]{:S(2)}) async-start(), calls=%async_computation.7 | async-start | bytes 5013504
  37.6 35.4 %copy-start.10 = (f32[8,1152]{1,0:T(8,128)}, f32[8,1152]{1,0:T(8,128)S(1)}, u32[]{:S(2)}) copy-start(f32[8,1152]{1,0:T(8,128)S(1)} %get-tuple-element.37) | copy-start | bytes 110596
  56.8 3.8 copy-start.2
  60.6 1.2 copy-start.11
  61.7 11.3 %copy-start.3 = (bf16[8,256,1152]{1,2,0:T(8,128)(2,1)}, bf16[8,256,1152]{1,2,0:T(8,128)(2,1)S(1)}, u32[]{:S(2)}) copy-start(bf16[8,256,1152]{1,2,0:T(8,128)(2,1)S(1)} %fusion.4) | copy-start | bytes 14155780
  72.0 6.8 %copy-start.4 = (f32[16,256,256]{1,2,0:T(8,128)}, f32[16,256,256]{1,2,0:T(8,128)S(1)}, u32[]{:S(2)}) copy-start(f32[16,256,256]{1,2,0:T(8,128)S(1)} %fusion.51) | copy-start | bytes 12582916
  72.0 1.4 copy-start.5
  73.4 8.7 %copy-start.8 = (bf16[72,1152]{1,0:T(8,128)(2,1)S(1)}, bf16[72,1152]{1,0:T(8,128)(2,1)}, u32[]{:S(2)}) copy-start(bf16[72,1152]{1,0:T(8,128)(2,1)} %param.23) | copy-start | bytes 497668
  93.7 2.1 copy-start.9
  95.8 11.0 %copy-start.16 = (bf16[8,256,72]{1,2,0:T(8,128)(2,1)}, bf16[8,256,72]{1,2,0:T(8,128)(2,1)S(1)}, u32[]{:S(2)}) copy-start(bf16[8,256,72]{1,2,0:T(8,128)(2,1)S(1)} %fusion.47) | copy-start | bytes 884740
  109.7 108.2 %all-gather.5.cloned.1.call-start = ((), (), s32[]{:S(2)}) async-start(), calls=%async_computation.6 | async-start | bytes 5013504 | tf_op jit(solution)/shard_map/all_gather | solution.py:194
  177.9 179.7 %all-reduce.3.cloned.1.call-start = ((), (), s32[]{:S(2)}) async-start(), calls=%async_computation.10 | async-start | bytes 221184
  234.9 6.7 %slice-start = ((s8[4718592]{0:T(1024)(128)(4,1)}), s8[4194304]{0:T(1024)(128)(4,1)S(1)}, s32[]{:S(2)}) async-start(s8[4718592]{0:T(1024)(128)(4,1)} %bitcast.203), calls=%async_computation.11 | async-start | bytes 8388608
  235.3 6.3 %slice-start.1 = ((s8[4718592]{0:T(1024)(128)(4,1)}), s8[524288]{0:T(1024)(128)(4,1)S(1)}, s32[]{:S(2)}) async-start(s8[4718592]{0:T(1024)(128)(4,1)} %bitcast.203), calls=%async_computation.12 | async-start | bytes 1048576
  235.3 6.3 %copy-start.17 = (bf16[8,256,72]{1,2,0:T(8,128)(2,1)S(1)}, bf16[8,256,72]{1,2,0:T(8,128)(2,1)}, u32[]{:S(2)}) copy-start(bf16[8,256,72]{1,2,0:T(8,128)(2,1)} %copy-done.16) | copy-start | bytes 884740
  235.3 268.2 %copy-start.1 = (bf16[1000,1152]{1,0:T(8,128)(2,1)S(1)}, bf16[1000,1152]{1,0:T(8,128)(2,1)}, u32[]{:S(2)}) copy-start(bf16[1000,1152]{1,0:T(8,128)(2,1)} %param.19) | copy-start | bytes 6912004
  241.6 11.7 %copy-start.15 = (u32[128]{0:T(128)S(1)}, u32[128]{0:T(128)}, u32[]{:S(2)}) copy-start(u32[128]{0:T(128)} %constant.33) | copy-start | bytes 1540
  243.9 183.0 %reduce-scatter.15.cloned.1.call-start = ((), (), s32[]{:S(2)}) async-start(), calls=%async_computation.9 | async-start | bytes 331776
  244.9 256.8 %reduce-scatter.13.cloned.1.call-start = ((), (), s32[]{:S(2)}) async-start(), calls=%async_computation.8 | async-start | bytes 663552
  246.7 140.0 %all-to-all-start.1 = ((bf16[8,8,144]{2,0,1:T(8,128)(2,1)}), bf16[8,8,144]{2,0,1:T(8,128)(2,1)S(1)}, u32[]{:S(2)}, u32[]{:S(2)}) async-start(bf16[8,8,144]{2,0,1:T(8,128)(2,1)} %copy.153), calls=%async_computation.1 | async-start | bytes 65536 | tf_op jit(solution)/shard_map/all_to_all | solution.py:221
Sparse Core Ops, SparseCore 0:
  9.7 47.0 all-gather.2
  109.8 66.2 reduce-scatter.10
  178.0 39.8 all-gather.4
  244.0 113.5 all-reduce.2
  361.1 65.7 reduce-scatter.14
  430.3 71.3 reduce-scatter.12

commit v2 on v0

v2 whole, which is shorter than its diff:
```python
import math

import jax
import jax.numpy as jnp
from jax import lax
from jax.experimental import pallas as pl
from jax.experimental.pallas import tpu as pltpu
from jax.sharding import PartitionSpec as P

HD = 72
HW = 3 * HD
norm_eps = 1e-06
F32 = jnp.float32
BF16 = jnp.bfloat16
MESH = pl.DeviceIdType.MESH


def lookup_rows(indices, table_rows):
    one_hot = (
        indices[:, None] == jnp.arange(table_rows.shape[0], dtype=jnp.int32)[None, :]
    ).astype(table_rows.dtype)
    return jnp.dot(one_hot, table_rows, preferred_element_type=F32)


def dot(a, b, ca, cb):
    return lax.dot_general(a, b, (((ca,), (cb,)), ((), ())), preferred_element_type=F32)


def make_kernel(n_t, n_dp, images, seq, norm_scale):
    chips = n_t // 2
    width = HD * n_t
    block = 2 * HD
    dp_rows = width // n_dp

    def kernel(
        noisy, mods, acts, wq_t, wq_s, wo_t, wo_s,
        gq_out, go_out, gm_out, act_out,
        noisy_g, mod_g, mod_i, wq_g, wo_g, wq_cat, wo_cat, wo_tr,
        normed, mod_s, mod_t, mixed, proj_s, prob, qkv_s,
        part, rs_in, cot, gp, gqkv, acc_q, acc_o, gmod, gm_in, gm_sum,
        pair_q, pair_o, pair_q_in, pair_o_in, dp_q, dp_o, dp_q_in, dp_o_in,
        s_ag, r_ag, s_mod, r_mod, s_w, r_w, s_act, r_act, l_sem,
        s_rs, r_rs, s_c, r_c, s_gm, r_gm, s_pair, r_pair,
        s_dq, r_dq, s_do, r_do, s_gd, r_gd,
    ):
        t = lax.axis_index("tensor")
        j = lax.axis_index("dp")
        chip = t // 2
        core = lax.rem(t, 2)
        mate = 1 - core
        mate_t = 2 * chip + mate

        barrier = pltpu.get_barrier_semaphore()
        for d in range(1, n_t):
            pl.semaphore_signal(
                barrier, inc=1, device_id={"tensor": lax.rem(t + d, n_t)}, device_id_type=MESH
            )
        for d in range(1, n_dp):
            pl.semaphore_signal(
                barrier, inc=1, device_id={"dp": lax.rem(j + d, n_dp)}, device_id_type=MESH
            )
        pl.semaphore_wait(barrier, n_t + n_dp - 2)

        def to_tensor(src, dst, ss, rs, peer):
            return pltpu.make_async_remote_copy(
                src_ref=src, dst_ref=dst, send_sem=ss, recv_sem=rs,
                device_id={"tensor": peer}, device_id_type=MESH,
            )

        def to_dp(src, dst, ss, rs, peer):
            return pltpu.make_async_remote_copy(
                src_ref=src, dst_ref=dst, send_sem=ss, recv_sem=rs,
                device_id={"dp": peer}, device_id_type=MESH,
            )

        def mod_copy(d):
            peer = lax.rem(t + d, n_t)
            return to_tensor(
                mods.at[lax.rem(peer, 2)], mod_g.at[t], s_mod.at[d], r_mod.at[d], peer
            )

        def ag_copy(i, d):
            peer = lax.rem(t + d, n_t)
            return to_tensor(
                noisy.at[images * lax.rem(peer, 2) + i], noisy_g.at[i, t],
                s_ag.at[i, d], r_ag.at[i, d], peer,
            )

        def w_copies():
            return [
                to_tensor(wq_t, wq_g.at[0, core], s_w.at[0], r_w.at[0], mate_t),
                to_tensor(wq_s, wq_g.at[1, core], s_w.at[1], r_w.at[1], mate_t),
                to_tensor(wo_t, wo_g.at[0, core], s_w.at[2], r_w.at[2], mate_t),
                to_tensor(wo_s, wo_g.at[1, core], s_w.at[3], r_w.at[3], mate_t),
            ]

        def act_copy(d):
            peer = lax.rem(j + d, n_dp)
            return to_dp(
                acts.at[pl.ds(pl.multiple_of(peer * dp_rows, 16), dp_rows)], act_out.at[j],
                s_act.at[d], r_act.at[d], peer,
            )

        locals_ = [
            pltpu.make_async_copy(mods.at[core], mod_g.at[t], l_sem.at[0]),
            pltpu.make_async_copy(wq_t, wq_g.at[0, core], l_sem.at[1]),
            pltpu.make_async_copy(wq_s, wq_g.at[1, core], l_sem.at[2]),
            pltpu.make_async_copy(wo_t, wo_g.at[0, core], l_sem.at[3]),
            pltpu.make_async_copy(wo_s, wo_g.at[1, core], l_sem.at[4]),
            pltpu.make_async_copy(
                acts.at[pl.ds(pl.multiple_of(j * dp_rows, 16), dp_rows)], act_out.at[j], l_sem.at[5]
            ),
        ]
        for i in range(images):
            locals_.append(
                pltpu.make_async_copy(
                    noisy.at[images * core + i], noisy_g.at[i, t], l_sem.at[6 + i]
                )
            )
        for copy in w_copies():
            copy.start()
        for d in range(1, n_t):
            mod_copy(d).start()
        for copy in locals_:
            copy.start()
        for i in range(images):
            for d in range(1, n_t):
                ag_copy(i, d).start()
        for d in range(1, n_dp):
            act_copy(d).start()

        for copy in locals_:
            copy.wait()
        for copy in w_copies():
            copy.wait_recv()
        for m in range(2):
            for h in range(2):
                flat = wq_g[m, h].astype(F32)
                wq_cat[m, HW * h : HW * (h + 1), :] = jnp.transpose(flat)
                wo_cat[m, HD * h : HD * (h + 1), :] = wo_g[m, h].astype(F32)
        for m in range(2):
            wo_tr[m] = jnp.transpose(wo_cat[m]).astype(BF16)

        for d in range(1, n_t):
            mod_copy(d).wait_recv()
        for src in range(n_t):
            piece = mod_g[src].astype(F32)
            for b in range(images):
                shifted = piece if b == 0 else pltpu.roll(piece, 128 - 16 * b, 1)
                mod_i[b, HD * src : HD * (src + 1), :] = shifted

        acc_q[...] = jnp.zeros_like(acc_q)
        acc_o[...] = jnp.zeros_like(acc_o)
        gmod[...] = jnp.zeros_like(gmod)

        def rs_copy(i, d):
            peer = lax.rem(chip + d, chips)
            return to_tensor(
                part.at[i, peer], rs_in.at[i, chip], s_rs.at[i, d], r_rs.at[i, d], 2 * peer + core
            )

        def cot_copy(i, d):
            peer = lax.rem(chip + d, chips)
            return to_tensor(
                cot.at[i, chip], cot.at[i, chip], s_c.at[i, d], r_c.at[i, d], 2 * peer + core
            )

        def scores_of(q, k):
            scores = dot(k, q, 0, 0) * (1.0 / math.sqrt(HD))
            exponent = jnp.exp(scores - jnp.max(scores, axis=0, keepdims=True))
            return exponent * (1.0 / jnp.sum(exponent, axis=0, keepdims=True))

        def forward(i):
            for d in range(1, n_t):
                peer = lax.rem(t + d, n_t)
                to_tensor(
                    noisy.at[0], noisy_g.at[i, lax.rem(t + n_t - d, n_t)],
                    s_ag.at[i, d], r_ag.at[i, d], peer,
                ).wait_recv()
            total = jnp.zeros((1, seq), F32)
            square = jnp.zeros((1, seq), F32)
            for src in range(n_t):
                x = noisy_g[i, src].astype(F32)
                total = total + jnp.sum(x, axis=0, keepdims=True)
                square = square + jnp.sum(x * x, axis=0, keepdims=True)
            mean = total * (1.0 / width)
            rstd = lax.rsqrt(square * (1.0 / width) - mean * mean + norm_eps)
            for c in range(chips):
                rows = slice(block * c, block * (c + 1))
                x = jnp.concatenate(
                    [noisy_g[i, 2 * c].astype(F32), noisy_g[i, 2 * c + 1].astype(F32)], axis=0
                )
                n = ((x - mean) * rstd).astype(BF16)
                normed[i, rows, :] = n
                n = n.astype(F32)
                for a in range(3):
                    shift = mod_i[i, rows, 3 * a : 3 * a + 1]
                    scale = mod_i[i, rows, 3 * a + 1 : 3 * a + 2]
                    value = (n * (1.0 + scale) + shift).astype(BF16)
                    if a == 2:
                        mod_s[i, rows, :] = value
                    else:
                        mod_t[a, rows, :] = value
            for a in range(3):
                weight = wq_cat[0 if a < 2 else 1].astype(BF16)
                act = mod_s[i] if a == 2 else mod_t[a]
                qkv = dot(weight, act, 1, 0)
                heads = []
                for h in range(2):
                    q, k, v = (
                        qkv[HW * h + HD * e : HW * h + HD * (e + 1)].astype(BF16) for e in range(3)
                    )
                    p = scores_of(q, k)
                    heads.append(dot(v, p.astype(BF16), 1, 0))
                    if a == 2:
                        prob[i, h] = p
                        for e, value in enumerate((q, k, v)):
                            qkv_s[i, h, e] = value
                mixed[a] = jnp.concatenate(heads, axis=0).astype(BF16)
            for h in range(2):
                mixed_h = mixed[2].astype(F32)[HD * h : HD * (h + 1)]
                gqkv[i, h, 0:HD, :] = mixed_h.astype(BF16)
            for c in range(chips):
                rows = slice(block * c, block * (c + 1))
                sums = jnp.zeros((block, seq), F32)
                for a in range(3):
                    value = dot(wo_tr[0 if a < 2 else 1, rows, :], mixed[a], 1, 0)
                    gate = mod_i[i, rows, 3 * a + 2 : 3 * a + 3]
                    if a == 2:
                        proj_s[i, rows, :] = value.astype(BF16)
                        gate = gate * norm_scale
                    sums = sums + value * gate
                part[i, c] = sums.astype(BF16)
            for d in range(1, chips):
                rs_copy(i, d).start()

        def reduce(i):
            for d in range(1, chips):
                rs_copy(i, d).wait_recv()
            sums = part[i, chip].astype(F32)
            for d in range(1, chips):
                sums = sums + rs_in[i, lax.rem(chip + d, chips)].astype(F32)
            cot[i, chip] = sums.astype(BF16)
            for d in range(1, chips):
                cot_copy(i, d).start()

        def backward(i):
            for d in range(1, chips):
                cot_copy(i, d).wait_recv()
            grads = []
            for c in range(chips):
                rows = slice(block * c, block * (c + 1))
                value = cot[i, c].astype(F32)
                gp[rows, :] = (value * mod_i[i, rows, 8:9]).astype(BF16)
                grads.append(
                    jnp.sum(value * proj_s[i, rows, :].astype(F32), axis=1, keepdims=True)
                )
            grad_gate = jnp.concatenate(grads, axis=0)
            grad_mixed = dot(wo_cat[1].astype(BF16), gp[...], 1, 0)
            grad_input = jnp.zeros((width, seq), F32)
            for h in range(2):
                low = grad_mixed[HD * h : HD * (h + 1)].astype(BF16)
                acc_o[h] += dot(gp[...], gqkv[i, h, 0:HD, :], 1, 1)
                q, k, v = (qkv_s[i, h, e] for e in range(3))
                p = prob[i, h]
                grad_prob = dot(v, low, 0, 0)
                delta = jnp.sum(p * grad_prob, axis=0, keepdims=True)
                ds = (p * (grad_prob - delta) * (1.0 / math.sqrt(HD))).astype(BF16)
                grad_q = dot(k, ds, 1, 0)
                grad_k = dot(q, ds, 1, 1)
                grad_v = dot(low, p.astype(BF16), 1, 1)
                gqkv[i, h] = jnp.concatenate([grad_q, grad_k, grad_v], axis=0).astype(BF16)
                grad_act = gqkv[i, h]
                acc_q[h] += dot(mod_s[i], grad_act, 1, 1)
                grad_input = grad_input + dot(wq_g[1, h], grad_act, 1, 0)
            grad_shift = jnp.sum(grad_input, axis=1, keepdims=True)
            grad_scale = jnp.sum(grad_input * normed[i].astype(F32), axis=1, keepdims=True)
            lane = lax.broadcasted_iota(jnp.int32, (width, 128), 1)
            gmod[...] += (
                jnp.where(lane == 4 * i, grad_shift, 0.0)
                + jnp.where(lane == 4 * i + 1, grad_scale, 0.0)
                + jnp.where(lane == 4 * i + 2, grad_gate, 0.0)
            )

        def forward_step(i, carry):
            forward(i)

            @pl.when(i > 0)
            def _():
                reduce(i - 1)

            return carry

        lax.fori_loop(0, images, forward_step, 0)

        def backward_step(i, carry):
            backward(i)

            @pl.when(i == 0)
            def _():
                reduce(images - 1)

            return carry

        lax.fori_loop(0, images, backward_step, 0)

        def gm_copy(d):
            peer = lax.rem(t + d, n_t)
            return to_tensor(
                gmod.at[pl.ds(pl.multiple_of(peer * HD, 8), HD)], gm_in.at[t],
                s_gm.at[d], r_gm.at[d], peer,
            )

        def pair_copies():
            return [
                to_tensor(pair_q, pair_q_in, s_pair.at[0], r_pair.at[0], mate_t),
                to_tensor(pair_o, pair_o_in, s_pair.at[1], r_pair.at[1], mate_t),
            ]

        def dp_copies(d):
            peer = lax.rem(j + d, n_dp)
            return [
                to_dp(dp_q.at[peer], dp_q_in.at[j], s_dq.at[d], r_dq.at[d], peer),
                to_dp(dp_o.at[peer], dp_o_in.at[j], s_do.at[d], r_do.at[d], peer),
            ]

        def gd_copy(d):
            peer = lax.rem(j + d, n_dp)
            return to_dp(gm_sum, gm_out.at[j], s_gd.at[d], r_gd.at[d], peer)

        pair_q[...] = acc_q[mate].astype(BF16)
        pair_o[...] = acc_o[mate].astype(BF16)
        for copy in pair_copies():
            copy.start()
        for d in range(1, n_t):
            gm_copy(d).start()
        for copy in pair_copies():
            copy.wait_recv()
        for s in range(n_dp):
            rows = slice(dp_rows * s, dp_rows * (s + 1))
            dp_q[s] = (acc_q[core, rows, :] + pair_q_in[rows, :].astype(F32)).astype(BF16)
            dp_o[s] = (acc_o[core, rows, :] + pair_o_in[rows, :].astype(F32)).astype(BF16)
        for d in range(1, n_dp):
            for copy in dp_copies(d):
                copy.start()
        for d in range(1, n_t):
            gm_copy(d).wait_recv()
        own = gmod[pl.ds(pl.multiple_of(t * HD, 8), HD), :]
        gm_in[t] = own
        even = gm_in[0]
        odd = gm_in[1]
        for c in range(1, chips):
            even = even + gm_in[2 * c]
            odd = odd + gm_in[2 * c + 1]
        both = even + pltpu.roll(odd, 4 * images, 1)
        gm_sum[...] = both
        gm_out[j] = both
        for d in range(1, n_dp):
            gd_copy(d).start()
        total_q = dp_q[j].astype(F32)
        total_o = dp_o[j].astype(F32)
        for d in range(1, n_dp):
            for copy in dp_copies(d):
                copy.wait_recv()
        for d in range(1, n_dp):
            src = lax.rem(j + d, n_dp)
            total_q = total_q + dp_q_in[src].astype(F32)
            total_o = total_o + dp_o_in[src].astype(F32)
        gq_out[...] = total_q
        go_out[...] = jnp.transpose(total_o)
        for d in range(1, n_dp):
            gd_copy(d).wait_recv()
            act_copy(d).wait_recv()

        for copy in w_copies() + pair_copies():
            copy.wait_send()
        for d in range(1, n_t):
            mod_copy(d).wait_send()
            gm_copy(d).wait_send()
            for i in range(images):
                ag_copy(i, d).wait_send()
        for d in range(1, chips):
            for i in range(images):
                rs_copy(i, d).wait_send()
                cot_copy(i, d).wait_send()
        for d in range(1, n_dp):
            act_copy(d).wait_send()
            gd_copy(d).wait_send()
            for copy in dp_copies(d):
                copy.wait_send()

    vm = pltpu.VMEM
    dma = pltpu.SemaphoreType.DMA
    scratch = [
        vm((images, n_t, HD, seq), BF16),
        vm((n_t, HD, 128), BF16),
        vm((images, width, 128), F32),
        vm((2, 2, width, HW), BF16),
        vm((2, 2, HD, width), BF16),
        vm((2, 2 * HW, width), F32),
        vm((2, 2 * HD, width), F32),
        vm((2, width, 2 * HD), BF16),
        vm((images, width, seq), BF16),
        vm((images, width, seq), BF16),
        vm((2, width, seq), BF16),
        vm((3, 2 * HD, seq), BF16),
        vm((images, width, seq), BF16),
        vm((images, 2, seq, seq), F32),
        vm((images, 2, 3, HD, seq), BF16),
        vm((images, chips, block, seq), BF16),
        vm((images, chips, block, seq), BF16),
        vm((images, chips, block, seq), BF16),
        vm((width, seq), BF16),
        vm((images, 2, HW, seq), BF16),
        vm((2, width, HW), F32),
        vm((2, width, HD), F32),
        vm((width, 128), F32),
        vm((n_t, HD, 128), F32),
        vm((HD, 128), F32),
        vm((width, HW), BF16),
        vm((width, HD), BF16),
        vm((width, HW), BF16),
        vm((width, HD), BF16),
        vm((n_dp, dp_rows, HW), BF16),
        vm((n_dp, dp_rows, HD), BF16),
        vm((n_dp, dp_rows, HW), BF16),
        vm((n_dp, dp_rows, HD), BF16),
        dma((images, n_t)),
        dma((images, n_t)),
        dma((n_t,)),
        dma((n_t,)),
        dma((4,)),
        dma((4,)),
        dma((n_dp,)),
        dma((n_dp,)),
        dma((6 + images,)),
        dma((images, chips)),
        dma((images, chips)),
        dma((images, chips)),
        dma((images, chips)),
        dma((n_t,)),
        dma((n_t,)),
        dma((2,)),
        dma((2,)),
        dma((n_dp,)),
        dma((n_dp,)),
        dma((n_dp,)),
        dma((n_dp,)),
        dma((n_dp,)),
        dma((n_dp,)),
    ]
    any_spec = pl.BlockSpec(memory_space=pl.ANY)
    vmem_spec = pl.BlockSpec(memory_space=pltpu.VMEM)
    return pl.pallas_call(
        kernel,
        out_shape=(
            jax.ShapeDtypeStruct((dp_rows, HW), F32),
            jax.ShapeDtypeStruct((HD, dp_rows), F32),
            jax.ShapeDtypeStruct((n_dp, HD, 128), F32),
            jax.ShapeDtypeStruct((n_dp, dp_rows, 128), BF16),
        ),
        in_specs=[any_spec] * 7,
        out_specs=(vmem_spec,) * 4,
        scratch_shapes=scratch,
        compiler_params=pltpu.CompilerParams(
            collective_id=0, has_side_effects=True, vmem_limit_bytes=60 * 1024 * 1024
        ),
        name="step",
    )


def local(
    noisy,
    labels,
    tsteps,
    guide_index,
    class_table,
    time_table,
    guide_table,
    guide_weights,
    teacher_qkv,
    teacher_out,
    teacher_ada,
    student_qkv,
    student_out,
    student_ada,
):
    samples, seq_len, width_part = noisy.shape
    n_t = lax.axis_size("tensor")
    n_dp = lax.axis_size("dp")
    images = samples // 2
    batch_size = samples * n_dp
    norm_scale = 1.0 / math.sqrt(batch_size * seq_len)
    null_class = class_table.shape[0] - 1
    time_embed = lookup_rows(tsteps, time_table)
    cond_embed = lookup_rows(labels, class_table) + time_embed
    null_embed = class_table[null_class].astype(F32)[None, :] + time_embed
    guide_hot = guide_index[:, None] == jnp.arange(guide_table.shape[0], dtype=jnp.int32)[None, :]
    student_embed = cond_embed + jnp.dot(
        guide_hot.astype(BF16), guide_table, preferred_element_type=F32
    )
    strength = jnp.sum(jnp.where(guide_hot, guide_weights[None, :], 0.0), axis=1)
    cond_act = jax.nn.silu(cond_embed).astype(BF16)
    null_act = jax.nn.silu(null_embed).astype(BF16)
    student_act = jax.nn.silu(student_embed).astype(BF16)
    teacher_act = jnp.concatenate([cond_act, null_act], axis=0)
    mod_t = jnp.einsum("bd,kde->bke", teacher_act, teacher_ada, preferred_element_type=F32)
    mod_s = jnp.einsum("bd,kde->bke", student_act, student_ada, preferred_element_type=F32)
    mods = jnp.stack([mod_t[:samples], mod_t[samples:], mod_s], axis=1)
    ones = jnp.ones_like(strength)
    factor = jnp.stack(
        [-(1.0 + strength) * norm_scale, strength * norm_scale, ones], axis=1
    )
    mods = jnp.concatenate([mods[:, :, :2], mods[:, :, 2:] * factor[:, :, None, None]], axis=2)
    mods = mods.reshape(2, images, 9, width_part)
    mods = jnp.pad(mods, ((0, 0), (0, 0), (0, 7), (0, 0))).reshape(2, images * 16, width_part)
    mods = jnp.pad(
        jnp.swapaxes(mods, 1, 2), ((0, 0), (0, 0), (0, 128 - images * 16))
    ).astype(BF16)
    acts = jnp.pad(student_act.T, ((0, 0), (0, 128 - samples)))
    step = make_kernel(n_t, n_dp, images, seq_len, norm_scale)
    grad_qkv, grad_out, gm, act_rows = step(
        jnp.swapaxes(noisy, 1, 2), mods, acts,
        teacher_qkv, student_qkv, teacher_out, student_out,
    )
    gm = gm[:, :, : 4 * samples].reshape(n_dp, width_part, samples, 4)[..., :3]
    grad_ada = jnp.einsum(
        "jdb,jebk->kde",
        act_rows[:, :, :samples].astype(F32),
        gm,
        precision=lax.Precision.HIGHEST,
    )
    return (grad_qkv, grad_out, grad_ada)


def solution(mesh):
    return jax.shard_map(
        local,
        mesh=mesh,
        in_specs=(
            P("dp", None, "tensor"),
            P("dp"),
            P("dp"),
            P("dp"),
            P(),
            P(),
            P(),
            P(),
            P(None, "tensor"),
            P("tensor", None),
            P(None, None, "tensor"),
            P(None, "tensor"),
            P("tensor", None),
            P(None, None, "tensor"),
        ),
        out_specs=(P("dp", "tensor"), P("tensor", "dp"), P(None, "dp", "tensor")),
        check_vma=False,
    )
```

time: 497 us -> 150 us (0.30)
  waiting for transfers between devices: 336 us -> 0 us
  Pallas kernels: 0 us -> 124 us
  matrix products: 57.8 us -> 4.82 us
  blocking collectives: 37 us -> 0 us
  local copies, waits for them, and re-layouts: 32.6 us -> 14 us
  between operations: 15.2 us -> 0.82 us
  other arithmetic: 12.4 us -> 4.26 us
    unnamed x10 -> x0, waiting for transfers between devices: 270 us -> none
    pallas_call x0 -> x1, Pallas kernels: none -> 124 us  [local(): step(jnp.swapaxes(noisy, 1, 2), mods, acts, teacher_qkv, student_qkv, tea...]
    all_gather x2 -> x0, waiting for transfers between devices: 65.8 us -> none  [the longest x1 40.1 us: local(): gathered = lax.all_gather(grad_proj, 'tensor', axis=2, tiled=True)]
    dot_general x20 -> x6, matrix products: 55.5 us -> 4.82 us  [the longest x2 1.58 us: lookup_rows(): return jnp.dot(one_hot, table_rows, preferred_element_type=F32)]
    all_to_all x3 -> x0, blocking collectives: 37 us -> none  [sent_to_all(): return lax.all_to_all(copies, axis, split_axis=0, concat_axis=0, tiled=True)]
    unnamed x43 -> x19, local copies, waits for them, and re-layouts: 19.9 us -> 6.1 us
    reshape x9 -> x2, local copies, waits for them, and re-layouts: 7.7 us -> 0.11 us  [the longest x1 0.1 us: local(): jnp.pad(mods, ((0, 0), (0, 0), (0, 7), (0, 0)))]
  transfers between devices with their start and end apart: 6 -> 0, of which waited for: 6 -> 0; matrix products, arithmetic and copies ran while one was open for 10% -> 0% of each run, Pallas kernels for 0% -> 0%
where the time goes in v2:
time: 150 us; the launch traced here: 148 us
  Pallas kernels  124 us (83%)
  local copies, waits for them, and re-layouts  14 us (9%)
  matrix products  4.82 us (3%)
  other arithmetic  4.26 us (3%)
    pallas_call x1, Pallas kernels, local(): step(jnp.swapaxes(noisy, 1, 2), mods, acts, teacher_qkv, student_qkv, tea...  124 us
    unnamed x19, local copies, waits for them, and re-layouts  6.1 us

profile of v2, /device:TPU:1, one launch (start us, length us, event | category | flops | bytes accessed | tf_op | source)
XLA Modules:
  0.0 147.7 jit_solution(1573101081036527434)
XLA Ops:
  0.6 0.0 copy-start
  0.6 0.0 copy-start.1
  0.7 0.0 copy-start.4
  0.7 1.0 select_reduce_fusion
  1.7 0.1 pad.21.clone
  1.8 0.1 maximum_maximum_fusion
  1.8 1.0 convert_reduce_fusion
  2.8 0.0 copy-done
  2.8 1.1 fusion.9
  3.9 0.0 copy-done.1
  3.9 0.0 copy-done.4
  3.9 0.5 convolution_add_fusion.1
  4.4 0.2 copy.80
  4.7 1.0 add_divide_fusion
  5.7 0.0 copy-start.6
  5.7 1.9 %copy.82 = f32[8,1152]{1,0:T(8,128)} copy(f32[8,1152]{0,1:T(8,128)} %get-tuple-element.26) | data formatting | bytes 73728 | tf_op jit(solution)/shard_map/jit(silu)/div | solution.py:504
  7.6 0.8 copy.81
  8.4 0.2 copy.77
  8.7 0.2 add_divide_fusion.1
  8.8 0.8 copy.78
  9.6 0.0 copy-start.5
  9.7 0.9 multiply_convert_fusion.2
  10.5 1.3 fusion.5
  11.8 0.0 copy-done.6
  11.9 1.3 fusion.3
  13.1 0.0 copy-start.2
  13.1 0.0 copy-start.3
  13.2 0.8 pad.16.acts
  13.9 0.0 copy-done.5
  13.9 0.4 convolution_bitcast_fusion.1
  14.3 0.1 fusion.12
  14.5 0.1 copy.87
  14.6 0.6 pad.15.mods
  15.3 0.0 copy-done.2
  15.3 1.1 copy.90.wq_t
  16.3 0.0 copy-done.3
  16.3 1.1 copy.91.wq_s
  17.4 123.8 %step.1 = (f32[144,216]{1,0:T(8,128)}, f32[72,144]{1,0:T(8,128)}, f32[8,72,128]{2,1,0:T(8,128)}, bf16[8,144,128]{2,1,0:T(8,128)(2,1)}) custom-call(bf16[8,72,256]{2,1,0:T(8,128)(2,1)} %bitcast.58, bf16[2,72,128]{2,1,0:T(8,128)(2,1)} %pad.15.mods, bf16[1152,128]{1,0:T(8,128)(2,1)} %pad.16.acts, bf16[1152,216]{1,0:T(8,128)(2,1)} %copy.90.wq_t, ...), custom_call_target="tpu_custom_call" | custom-call | tf_op jit(solution)/shard_map/step/pallas_call | solution.py:522
  141.2 1.1 copy.94
  142.3 1.1 copy.92
  143.4 0.3 convolution_bitcast_fusion
  143.7 0.8 copy.95
  144.6 1.6 %copy.103 = f32[144,216]{1,0:T(8,128)} copy(f32[144,216]{1,0:T(8,128)} %get-tuple-element.39) | data formatting | bytes 248832
  146.1 1.5 %copy.104 = f32[72,144]{1,0:T(8,128)} copy(f32[72,144]{1,0:T(8,128)} %get-tuple-element.40) | data formatting | bytes 82944
  (7 shorter events, 0.1 us)
Async XLA Ops:
  0.6 2.2 %copy-start = (bf16[1000,1152]{1,0:T(8,128)(2,1)S(1)}, bf16[1000,1152]{1,0:T(8,128)(2,1)}, u32[]{:S(2)}) copy-start(bf16[1000,1152]{1,0:T(8,128)(2,1)} %param.19) | copy-start | bytes 6912004
  0.6 3.3 %copy-start.1 = (bf16[1001,1152]{1,0:T(8,128)(2,1)S(1)}, bf16[1001,1152]{1,0:T(8,128)(2,1)}, u32[]{:S(2)}) copy-start(bf16[1001,1152]{1,0:T(8,128)(2,1)} %param.18) | copy-start | bytes 6918916
  0.7 3.3 %copy-start.4 = (s32[8]{0:T(128)S(1)}, s32[8]{0:T(128)}, u32[]{:S(2)}) copy-start(s32[8]{0:T(128)} %param.15) | copy-start | bytes 100
  5.7 6.2 %copy-start.6 = (s32[8]{0:T(128)S(1)}, s32[8]{0:T(128)}, u32[]{:S(2)}) copy-start(s32[8]{0:T(128)} %param.17) | copy-start | bytes 100
  9.6 4.3 %copy-start.5 = (bf16[3,1152,72]{1,2,0:T(8,128)(2,1)S(1)}, bf16[3,1152,72]{1,2,0:T(8,128)(2,1)}, u32[]{:S(2)}) copy-start(bf16[3,1152,72]{1,2,0:T(8,128)(2,1)} %param.27) | copy-start | bytes 1492996
  13.1 2.1 %copy-start.2 = (bf16[1152,216]{0,1:T(8,128)(2,1)S(1)}, bf16[1152,216]{0,1:T(8,128)(2,1)}, u32[]{:S(2)}) copy-start(bf16[1152,216]{0,1:T(8,128)(2,1)} %param.22) | copy-start | bytes 1492996
  13.1 3.2 %copy-start.3 = (bf16[1152,216]{0,1:T(8,128)(2,1)S(1)}, bf16[1152,216]{0,1:T(8,128)(2,1)}, u32[]{:S(2)}) copy-start(bf16[1152,216]{0,1:T(8,128)(2,1)} %param.25) | copy-start | bytes 1492996

commit v3 on v2

v3 whole, which is shorter than its diff:
```python
import math

import jax
import jax.numpy as jnp
from jax import lax
from jax.experimental import pallas as pl
from jax.experimental.pallas import tpu as pltpu
from jax.sharding import PartitionSpec as P

HD = 72
HW = 3 * HD
HP = 80
norm_eps = 1e-06
F32 = jnp.float32
BF16 = jnp.bfloat16
MESH = pl.DeviceIdType.MESH
SPLIT = 40


def dot(a, b, ca, cb):
    return lax.dot_general(a, b, (((ca,), (cb,)), ((), ())), preferred_element_type=F32)


def iota(shape, dim):
    return lax.broadcasted_iota(jnp.int32, shape, dim)


def make_kernel(n_t, n_dp, samples, seq, norm_scale):
    chips = n_t // 2
    n_x = chips // 2
    images = samples // 2
    width = HD * n_t
    block = 2 * HD
    dp_rows = width // n_dp
    groups = HD // 8

    def kernel(
        labels, tsteps, guides, strengths,
        noisy, tab_c, tab_t, tab_g, wq_t, wq_s, wo_t, wo_s, ada_t, ada_s,
        gq_out, go_out, ga_out,
        noisy_p, noisy_g, c_tab, t_tab, g_tab, a_tab, mods, mod_g, mod_i, acts, act_g,
        wq_g, wo_g, wq_cat, wq_tr, wo_cat, wo_tr,
        normed, mod_s, mod_t, mixed, mixed_s, proj_s, prob, qkv_s,
        part, rs_in, cot, gp, gqkv, acc_q, acc_o, gmod, gm_send, gm_in, gm_sum, gm_all,
        pair_q, pair_o, pair_q_in, pair_o_in, dp_q, dp_o, dp_q_in, dp_o_in,
        l_sem, s_n, r_n, s_w, r_w, s_mod, r_mod, s_act, r_act,
        s_ag, r_ag, s_rs, r_rs, s_c, r_c, s_gm, r_gm, s_pair, r_pair,
        s_dq, r_dq, s_do, r_do, s_gd, r_gd,
    ):
        t = lax.axis_index("tensor")
        j = lax.axis_index("dp")
        chip = t // 2
        core = lax.rem(t, 2)
        x = chip // 2
        z = lax.rem(chip, 2)
        mate = 1 - core
        mate_t = 2 * chip + mate
        chip_z = 2 * x + 1 - z

        loads = [
            pltpu.make_async_copy(tab_c, c_tab, l_sem.at[0]),
            pltpu.make_async_copy(tab_t, t_tab, l_sem.at[1]),
            pltpu.make_async_copy(tab_g, g_tab, l_sem.at[2]),
            pltpu.make_async_copy(ada_t, a_tab.at[0], l_sem.at[3]),
            pltpu.make_async_copy(ada_s, a_tab.at[1], l_sem.at[4]),
            pltpu.make_async_copy(wq_t, wq_g.at[0, core], l_sem.at[5]),
            pltpu.make_async_copy(wq_s, wq_g.at[1, core], l_sem.at[6]),
            pltpu.make_async_copy(wo_t, wo_g.at[0, core], l_sem.at[7]),
            pltpu.make_async_copy(wo_s, wo_g.at[1, core], l_sem.at[8]),
        ]
        own_noisy = pltpu.make_async_copy(
            noisy.at[pl.ds(images * core, images)], noisy_p.at[core], l_sem.at[9]
        )
        own_noisy.start()
        for copy in loads:
            copy.start()

        barrier = pltpu.get_barrier_semaphore()
        for d in range(1, n_t):
            pl.semaphore_signal(
                barrier, inc=1, device_id={"tensor": lax.rem(t + d, n_t)}, device_id_type=MESH
            )
        for d in range(1, n_dp):
            pl.semaphore_signal(
                barrier, inc=1, device_id={"dp": lax.rem(j + d, n_dp)}, device_id_type=MESH
            )
        pl.semaphore_wait(barrier, n_t + n_dp - 2)

        def to_tensor(src, dst, ss, rs, peer):
            return pltpu.make_async_remote_copy(
                src_ref=src, dst_ref=dst, send_sem=ss, recv_sem=rs,
                device_id={"tensor": peer}, device_id_type=MESH,
            )

        def to_dp(src, dst, ss, rs, peer):
            return pltpu.make_async_remote_copy(
                src_ref=src, dst_ref=dst, send_sem=ss, recv_sem=rs,
                device_id={"dp": peer}, device_id_type=MESH,
            )

        def x_chip(d):
            return 2 * lax.rem(x + d, n_x) + z

        def device_of(c):
            return 2 * c + core

        def gather_z(buf, i, ss, rs):
            own = buf.at[i, chip]
            first = [to_tensor(own, own, ss.at[i, 0], rs.at[i, 0], device_of(chip_z))]
            first += [
                to_tensor(own, own, ss.at[i, d], rs.at[i, d], device_of(x_chip(d)))
                for d in range(1, n_x)
            ]
            other = buf.at[i, chip_z]
            second = [
                to_tensor(other, other, ss.at[i, n_x + d], rs.at[i, n_x + d], device_of(x_chip(d)))
                for d in range(1, n_x)
            ]
            return first, second, first[:1]

        def gather_x(buf, i, ss, rs):
            own = buf.at[i, chip]
            first = [
                to_tensor(own, own, ss.at[i, d], rs.at[i, d], device_of(x_chip(d)))
                for d in range(1, n_x)
            ]
            ahead = len(first)
            first.append(to_tensor(own, own, ss.at[i, n_x], rs.at[i, n_x], device_of(chip_z)))
            second = []
            for d in range(1, n_x):
                other = buf.at[i, 2 * lax.rem(x + n_x - d, n_x) + z]
                second.append(
                    to_tensor(
                        other, other, ss.at[i, n_x + d], rs.at[i, n_x + d], device_of(chip_z)
                    )
                )
            return first, second, first[:ahead]

        def by_parity(i, even, odd):
            @pl.when(lax.rem(i, 2) == 0)
            def _():
                even()

            @pl.when(lax.rem(i, 2) == 1)
            def _():
                odd()

        def gather_start(buf, i, ss, rs):
            def run(form):
                for copy in form(buf, i, ss, rs)[0]:
                    copy.start()

            by_parity(i, lambda: run(gather_z), lambda: run(gather_x))

        def gather_pass(buf, i, ss, rs):
            def run(form):
                _, second, needed = form(buf, i, ss, rs)
                for copy in needed:
                    copy.wait_recv()
                for copy in second:
                    copy.start()

            by_parity(i, lambda: run(gather_z), lambda: run(gather_x))

        def gather_end(buf, i, ss, rs):
            def run(form):
                first, second, needed = form(buf, i, ss, rs)
                for copy in first + second:
                    if not any(copy is other for other in needed):
                        copy.wait_recv()

            by_parity(i, lambda: run(gather_z), lambda: run(gather_x))

        def sum_z(i):
            first = [
                to_tensor(
                    part.at[i, 2 * e + 1 - z], rs_in.at[i, e],
                    s_rs.at[i, e], r_rs.at[i, e], device_of(chip_z),
                )
                for e in range(n_x)
            ]
            second = [
                to_tensor(
                    part.at[i, x_chip(d)], rs_in.at[i, n_x + d],
                    s_rs.at[i, n_x + d], r_rs.at[i, n_x + d], device_of(x_chip(d)),
                )
                for d in range(1, n_x)
            ]
            return first, second

        def sum_x(i):
            first = [
                to_tensor(
                    part.at[i, pl.ds(2 * lax.rem(x + d, n_x), 2)], rs_in.at[i, pl.ds(2 * d, 2)],
                    s_rs.at[i, d], r_rs.at[i, d], device_of(x_chip(d)),
                )
                for d in range(1, n_x)
            ]
            second = [
                to_tensor(
                    part.at[i, chip_z], rs_in.at[i, 0], s_rs.at[i, 0], r_rs.at[i, 0],
                    device_of(chip_z),
                )
            ]
            return first, second

        def sum_start(i):
            def run(form):
                for copy in form(i)[0]:
                    copy.start()

            by_parity(i, lambda: run(sum_z), lambda: run(sum_x))

        def sum_pass(i):
            def even():
                first, second = sum_z(i)
                for copy in first:
                    copy.wait_recv()
                for d in range(1, n_x):
                    e = lax.rem(x + d, n_x)
                    total = part[i, 2 * e + z].astype(F32) + rs_in[i, e].astype(F32)
                    part[i, 2 * e + z] = total.astype(BF16)
                for copy in second:
                    copy.start()

            def odd():
                first, second = sum_x(i)
                for copy in first:
                    copy.wait_recv()
                total = part[i, chip_z].astype(F32)
                for d in range(1, n_x):
                    total = total + rs_in[i, 2 * d + 1 - z].astype(F32)
                part[i, chip_z] = total.astype(BF16)
                for copy in second:
                    copy.start()

            by_parity(i, even, odd)

        def sum_end(i):
            def even():
                for copy in sum_z(i)[1]:
                    copy.wait_recv()
                total = part[i, chip].astype(F32) + rs_in[i, x].astype(F32)
                for d in range(1, n_x):
                    total = total + rs_in[i, n_x + d].astype(F32)
                cot[i, chip] = total.astype(BF16)

            def odd():
                for copy in sum_x(i)[1]:
                    copy.wait_recv()
                total = part[i, chip].astype(F32) + rs_in[i, 0].astype(F32)
                for d in range(1, n_x):
                    total = total + rs_in[i, 2 * d + z].astype(F32)
                cot[i, chip] = total.astype(BF16)

            by_parity(i, even, odd)

        mate_noisy = to_tensor(
            noisy.at[pl.ds(images * mate, images)], noisy_p.at[core], s_n.at[0], r_n.at[0], mate_t
        )
        w_copies = [
            to_tensor(wq_t, wq_g.at[0, core], s_w.at[0], r_w.at[0], mate_t),
            to_tensor(wq_s, wq_g.at[1, core], s_w.at[1], r_w.at[1], mate_t),
            to_tensor(wo_t, wo_g.at[0, core], s_w.at[2], r_w.at[2], mate_t),
            to_tensor(wo_s, wo_g.at[1, core], s_w.at[3], r_w.at[3], mate_t),
        ]
        mate_noisy.start()
        for copy in w_copies:
            copy.start()
        own_noisy.wait()
        mate_noisy.wait_recv()
        for i in range(images):
            both = jnp.concatenate(
                [noisy_p[0, i].astype(F32), noisy_p[1, i].astype(F32)], axis=0
            )
            noisy_g[i, chip] = both.astype(BF16)
        for i in range(min(2, images)):
            gather_start(noisy_g, i, s_ag, r_ag)

        for copy in loads[:5]:
            copy.wait()

        def one_hot(ref, size):
            row = iota((samples, size), 0)
            lane = iota((samples, size), 1)
            hot = jnp.zeros((samples, size), F32)
            for b in range(samples):
                hot = jnp.where((row == b) & (lane == ref[b]), 1.0, hot)
            return hot.astype(BF16)

        def lookup(ref, table, size):
            whole = size // 16 * 16
            hot = one_hot(ref, whole + 16)
            last = table[whole:size, :].astype(F32)
            last = jnp.concatenate([last, jnp.zeros((16 - size + whole, width), F32)], axis=0)
            return dot(hot[:, :whole], table[0:whole, :], 1, 0) + dot(
                hot[:, whole:], last.astype(BF16), 1, 0
            )

        time_embed = lookup(tsteps, t_tab, tab_t.shape[0])
        classes = tab_c.shape[0] - 1
        cond_embed = lookup(labels, c_tab, classes) + time_embed
        null_row = c_tab[classes - 8 :, :].astype(F32)[8:9]
        null_embed = null_row + time_embed
        student_embed = cond_embed + dot(one_hot(guides, tab_g.shape[0]), g_tab[...], 1, 0)

        def silu(v):
            return v / (1.0 + jnp.exp(-v))

        student_act = silu(student_embed)
        teacher_act = jnp.concatenate([silu(cond_embed), silu(null_embed)], axis=0).astype(BF16)
        acts[...] = jnp.zeros_like(acts)
        acts[:, 0:samples] = jnp.transpose(student_act).astype(BF16)
        student_act = jnp.concatenate([student_act, jnp.zeros_like(student_act)], axis=0).astype(BF16)
        lane_t = iota((1, 2 * samples), 1)
        factor = jnp.zeros((1, 2 * samples), F32)
        for b in range(samples):
            strength = strengths[guides[b]]
            factor = jnp.where(lane_t == b, -(1.0 + strength) * norm_scale, factor)
            factor = jnp.where(lane_t == samples + b, strength * norm_scale, factor)
        spread = jnp.zeros((HD, 256), F32)
        for k in range(3):
            value_t = dot(a_tab[0, k], teacher_act, 1, 1)
            value_s = dot(a_tab[1, k], student_act, 1, 1)
            if k == 2:
                value_t = value_t * factor
            for first, value in ((0, value_t), (2, value_s)):
                row = iota((2 * samples, 256), 0)
                lane = iota((2 * samples, 256), 1)
                b = lax.rem(row, samples)
                kind = first + row // samples
                target = 128 * (b // images) + 16 * lax.rem(b, images) + 3 * kind + k
                hot = jnp.where((lane == target) & (kind < 3), 1.0, 0.0).astype(BF16)
                spread = spread + dot(value.astype(BF16), hot, 1, 0)
        for kk in range(2):
            half = spread[:, 128 * kk : 128 * (kk + 1)]
            low = jnp.concatenate(
                [pltpu.roll(half[SPLIT:], 64, 1), jnp.zeros((2 * SPLIT - HD, 128), F32)], axis=0
            )
            mods[kk] = (half[:SPLIT] + low).astype(BF16)

        def mod_copy(d):
            peer = lax.rem(t + d, n_t)
            return to_tensor(
                mods.at[lax.rem(peer, 2)], mod_g.at[t], s_mod.at[d], r_mod.at[d], peer
            )

        def act_copy(d):
            peer = lax.rem(j + d, n_dp)
            return to_dp(
                acts.at[pl.ds(pl.multiple_of(peer * dp_rows, 16), dp_rows)], act_g.at[j],
                s_act.at[d], r_act.at[d], peer,
            )

        for d in range(1, n_t):
            mod_copy(d).start()
        gather_pass(noisy_g, 0, s_ag, r_ag)
        if images > 2:
            gather_start(noisy_g, 2, s_ag, r_ag)
        for d in range(1, n_dp):
            act_copy(d).start()
        mod_g[t] = mods[core]
        act_g[j] = acts[pl.ds(pl.multiple_of(j * dp_rows, 16), dp_rows), :]

        for copy in loads[5:]:
            copy.wait()
        for copy in w_copies:
            copy.wait_recv()
        for m in range(2):
            both = jnp.concatenate([wq_g[m, 0].astype(F32), wq_g[m, 1].astype(F32)], axis=0)
            wq_cat[m] = both.astype(BF16)
            if m == 1:
                wq_tr[...] = jnp.transpose(both).astype(BF16)
            both = jnp.concatenate([wo_g[m, 0].astype(F32), wo_g[m, 1].astype(F32)], axis=0)
            if m == 1:
                wo_cat[...] = both.astype(BF16)
            wo_tr[m] = jnp.transpose(both).astype(BF16)
        acc_q[...] = jnp.zeros_like(acc_q)
        acc_o[...] = jnp.zeros_like(acc_o)
        gmod[...] = jnp.zeros_like(gmod)
        gather_pass(noisy_g, 1, s_ag, r_ag)
        if images > 3:
            gather_start(noisy_g, 3, s_ag, r_ag)

        for d in range(1, n_t):
            mod_copy(d).wait_recv()
        for src in range(n_t):
            piece = mod_g[src].astype(F32)
            for b in range(images):
                near = piece if b == 0 else pltpu.roll(piece, 128 - 16 * b, 1)
                far = pltpu.roll(piece, 64 - 16 * b, 1)
                mod_i[b, HD * src : HD * src + SPLIT, :] = near
                mod_i[b, HD * src + SPLIT : HD * (src + 1), :] = far[: HD - SPLIT]

        def padded(value):
            rows = jnp.zeros((HP - HD, seq), F32)
            return jnp.concatenate([value, rows], axis=0).astype(BF16)

        def attend(q, k, v):
            scores = dot(k, q, 0, 0) * (1.0 / math.sqrt(HD))
            exponent = jnp.exp(scores - jnp.max(scores, axis=0, keepdims=True))
            p = exponent * (1.0 / jnp.sum(exponent, axis=0, keepdims=True))
            return p, dot(v, p.astype(BF16), 1, 0)[:HD]

        def forward_in(i):
            gather_end(noisy_g, i, s_ag, r_ag)
            total = jnp.zeros((1, seq), F32)
            square = jnp.zeros((1, seq), F32)
            for c in range(chips):
                value = noisy_g[i, c].astype(F32)
                total = total + jnp.sum(value, axis=0, keepdims=True)
                square = square + jnp.sum(value * value, axis=0, keepdims=True)
            mean = total * (1.0 / width)
            rstd = lax.rsqrt(square * (1.0 / width) - mean * mean + norm_eps)
            for c in range(chips):
                rows = slice(block * c, block * (c + 1))
                n = ((noisy_g[i, c].astype(F32) - mean) * rstd).astype(BF16)
                normed[i, rows, :] = n
                n = n.astype(F32)
                for a in range(3):
                    shift = mod_i[i, rows, 3 * a : 3 * a + 1]
                    scale = mod_i[i, rows, 3 * a + 1 : 3 * a + 2]
                    value = (n * (1.0 + scale) + shift).astype(BF16)
                    if a == 2:
                        mod_s[i, rows, :] = value
                    else:
                        mod_t[a, rows, :] = value

        def forward_model(i, a):
            act = mod_s[i] if a == 2 else mod_t[a]
            qkv = dot(wq_cat[0 if a < 2 else 1], act, 1, 0)
            heads = []
            for h in range(2):
                q, k, v = (
                    padded(qkv[HW * h + HD * e : HW * h + HD * (e + 1)]) for e in range(3)
                )
                p, mix = attend(q, k, v)
                heads.append(mix)
                if a == 2:
                    prob[i, h] = p
                    mixed_s[i, h] = mix.astype(BF16)
                    for e, value in enumerate((q, k, v)):
                        qkv_s[i, h, e] = value
            mixed[a] = jnp.concatenate(heads, axis=0).astype(BF16)

        def forward_out(i):
            for c in range(chips):
                rows = slice(block * c, block * (c + 1))
                sums = jnp.zeros((block, seq), F32)
                for a in range(3):
                    value = dot(wo_tr[0 if a < 2 else 1, rows, :], mixed[a], 1, 0)
                    gate = mod_i[i, rows, 3 * a + 2 : 3 * a + 3]
                    if a == 2:
                        proj_s[i, rows, :] = value.astype(BF16)
                        gate = gate * norm_scale
                    sums = sums + value * gate
                part[i, c] = sums.astype(BF16)
            sum_start(i)

        def backward_in(i):
            gather_end(cot, i, s_c, r_c)
            grads = []
            for c in range(chips):
                rows = slice(block * c, block * (c + 1))
                value = cot[i, c].astype(F32)
                gp[rows, :] = (value * mod_i[i, rows, 8:9]).astype(BF16)
                grads.append(
                    jnp.sum(value * proj_s[i, rows, :].astype(F32), axis=1, keepdims=True)
                )
            grad_gate = jnp.concatenate(grads, axis=0)
            lane = iota((width, 128), 1)
            gmod[...] += jnp.where(lane == 8 + i, grad_gate, 0.0)
            grad_mixed = dot(wo_cat[...], gp[...], 1, 0)
            acts_grad = []
            for h in range(2):
                low = padded(grad_mixed[HD * h : HD * (h + 1)])
                acc_o[h] += dot(gp[...], mixed_s[i, h], 1, 1)
                q, k, v = (qkv_s[i, h, e] for e in range(3))
                p = prob[i, h]
                grad_prob = dot(v, low, 0, 0)
                delta = jnp.sum(p * grad_prob, axis=0, keepdims=True)
                ds = (p * (grad_prob - delta) * (1.0 / math.sqrt(HD))).astype(BF16)
                acts_grad.append(dot(k, ds, 1, 0)[:HD])
                acts_grad.append(dot(q, ds, 1, 1)[:HD])
                acts_grad.append(dot(low, p.astype(BF16), 1, 1)[:HD])
            gqkv[...] = jnp.concatenate(acts_grad, axis=0).astype(BF16)
            for h in range(2):
                head = jnp.concatenate(acts_grad[3 * h : 3 * h + 3], axis=0).astype(BF16)
                acc_q[h] += dot(mod_s[i], head, 1, 1)

        def backward_out(i):
            shifts = []
            scales = []
            for c in range(chips):
                rows = slice(block * c, block * (c + 1))
                value = dot(wq_tr[rows, :], gqkv[...], 1, 0)
                shifts.append(jnp.sum(value, axis=1, keepdims=True))
                scales.append(
                    jnp.sum(value * normed[i, rows, :].astype(F32), axis=1, keepdims=True)
                )
            lane = iota((width, 128), 1)
            gmod[...] += jnp.where(lane == i, jnp.concatenate(shifts, axis=0), 0.0) + jnp.where(
                lane == 4 + i, jnp.concatenate(scales, axis=0), 0.0
            )

        def forward_step(i, carry):
            forward_in(i)

            @pl.when(i < images - 2)
            def _():
                gather_pass(noisy_g, i + 2, s_ag, r_ag)

            forward_model(i, 0)

            @pl.when(i > 0)
            def _():
                sum_pass(i - 1)

            forward_model(i, 1)

            @pl.when(i > 1)
            def _():
                gather_pass(cot, i - 2, s_c, r_c)

            forward_model(i, 2)

            @pl.when(i > 0)
            def _():
                sum_end(i - 1)
                gather_start(cot, i - 1, s_c, r_c)

            forward_out(i)
            return carry

        lax.fori_loop(0, images, forward_step, 0)
        if images > 1:
            gather_pass(cot, images - 2, s_c, r_c)
        sum_pass(images - 1)

        def backward_step(i, carry):
            backward_in(i)

            @pl.when(i == 0)
            def _():
                sum_end(images - 1)
                gather_start(cot, images - 1, s_c, r_c)

            backward_out(i)

            @pl.when(i == 0)
            def _():
                gather_pass(cot, images - 1, s_c, r_c)

            return carry

        lax.fori_loop(0, images, backward_step, 0)

        def gm_copy(d):
            peer = lax.rem(t + d, n_t)
            return to_tensor(gm_send.at[peer], gm_in.at[t], s_gm.at[d], r_gm.at[d], peer)

        pair_copies = [
            to_tensor(pair_q, pair_q_in, s_pair.at[0], r_pair.at[0], mate_t),
            to_tensor(pair_o, pair_o_in, s_pair.at[1], r_pair.at[1], mate_t),
        ]

        def dp_copies(d):
            peer = lax.rem(j + d, n_dp)
            return [
                to_dp(dp_q.at[peer], dp_q_in.at[j], s_dq.at[d], r_dq.at[d], peer),
                to_dp(dp_o.at[peer], dp_o_in.at[j], s_do.at[d], r_do.at[d], peer),
            ]

        def gd_copy(d):
            peer = lax.rem(j + d, n_dp)
            return to_dp(gm_sum, gm_all.at[j], s_gd.at[d], r_gd.at[d], peer)

        pair_q[...] = acc_q[mate].astype(BF16)
        pair_o[...] = acc_o[mate].astype(BF16)
        for copy in pair_copies:
            copy.start()
        for src in range(n_t):
            packed = gmod[HD * src : HD * src + 8, :]
            for g in range(1, groups):
                rows = slice(HD * src + 8 * g, HD * src + 8 * (g + 1))
                packed = packed + pltpu.roll(gmod[rows, :], 12 * g, 1)
            gm_send[src] = packed
        for d in range(1, n_t):
            gm_copy(d).start()
        gm_in[t] = gm_send[t]
        for copy in pair_copies:
            copy.wait_recv()
        for s in range(n_dp):
            rows = slice(dp_rows * s, dp_rows * (s + 1))
            dp_q[s] = (acc_q[core, rows, :] + pair_q_in[rows, :].astype(F32)).astype(BF16)
            dp_o[s] = (acc_o[core, rows, :] + pair_o_in[rows, :].astype(F32)).astype(BF16)
        for d in range(1, n_dp):
            for copy in dp_copies(d):
                copy.start()
        for d in range(1, n_t):
            gm_copy(d).wait_recv()
        for kk in range(2):
            total = gm_in[kk]
            for c in range(1, chips):
                total = total + gm_in[2 * c + kk]
            gm_sum[kk] = total
        for d in range(1, n_dp):
            gd_copy(d).start()
        gm_all[j] = gm_sum[...]
        for d in range(1, n_dp):
            act_copy(d).wait_recv()
        rows_act = act_g[0].astype(F32)
        for s in range(1, n_dp):
            rows_act = rows_act + pltpu.roll(act_g[s].astype(F32), samples * s, 1)

        total_q = dp_q[j].astype(F32)
        total_o = dp_o[j].astype(F32)
        for d in range(1, n_dp):
            for copy in dp_copies(d):
                copy.wait_recv()
        for d in range(1, n_dp):
            src = lax.rem(j + d, n_dp)
            total_q = total_q + dp_q_in[src].astype(F32)
            total_o = total_o + dp_o_in[src].astype(F32)
        gq_out[...] = total_q
        go_out[...] = jnp.transpose(total_o)

        for d in range(1, n_dp):
            gd_copy(d).wait_recv()
        lane = iota((8, 128), 1)
        for k in range(3):
            pieces = []
            for g in range(groups):
                value = jnp.zeros((8, 128), F32)
                for s in range(n_dp):
                    for kk in range(2):
                        at = samples * s + images * kk
                        shift = (at - 12 * g - 4 * k) % 128
                        moved = gm_all[s, kk]
                        if shift:
                            moved = pltpu.roll(moved, shift, 1)
                        value = jnp.where((lane >= at) & (lane < at + images), moved, value)
                pieces.append(value)
            ga_out[k] = lax.dot_general(
                rows_act, jnp.concatenate(pieces, axis=0), (((1,), (1,)), ((), ())),
                precision=lax.Precision.HIGHEST, preferred_element_type=F32,
            )

        mate_noisy.wait_send()
        for copy in w_copies + pair_copies:
            copy.wait_send()
        for d in range(1, n_t):
            mod_copy(d).wait_send()
            gm_copy(d).wait_send()
        for d in range(1, n_dp):
            act_copy(d).wait_send()
            gd_copy(d).wait_send()
            for copy in dp_copies(d):
                copy.wait_send()
        for i in range(images):
            form = gather_z if i % 2 == 0 else gather_x
            sums = sum_z(i) if i % 2 == 0 else sum_x(i)
            for copy in (
                sum(form(noisy_g, i, s_ag, r_ag)[:2], [])
                + sum(form(cot, i, s_c, r_c)[:2], [])
                + sum(sums, [])
            ):
                copy.wait_send()

    vm = pltpu.VMEM
    dma = pltpu.SemaphoreType.DMA
    scratch = [
        vm((2, images, HD, seq), BF16),
        vm((images, chips, block, seq), BF16),
        vm((1001, width), BF16),
        vm((1000, width), BF16),
        vm((32, width), BF16),
        vm((2, 3, HD, width), BF16),
        vm((2, SPLIT, 128), BF16),
        vm((n_t, SPLIT, 128), BF16),
        vm((images, width, 128), F32),
        vm((width, 128), BF16),
        vm((n_dp, dp_rows, 128), BF16),
        vm((2, 2, HW, width), BF16),
        vm((2, 2, HD, width), BF16),
        vm((2, 2 * HW, width), BF16),
        vm((width, 2 * HW), BF16),
        vm((2 * HD, width), BF16),
        vm((2, width, 2 * HD), BF16),
        vm((images, width, seq), BF16),
        vm((images, width, seq), BF16),
        vm((2, width, seq), BF16),
        vm((3, 2 * HD, seq), BF16),
        vm((images, 2, HD, seq), BF16),
        vm((images, width, seq), BF16),
        vm((images, 2, seq, seq), F32),
        vm((images, 2, 3, HP, seq), BF16),
        vm((images, chips, block, seq), BF16),
        vm((images, 2 * n_x, block, seq), BF16),
        vm((images, chips, block, seq), BF16),
        vm((width, seq), BF16),
        vm((2 * HW, seq), BF16),
        vm((2, width, HW), F32),
        vm((2, width, HD), F32),
        vm((width, 128), F32),
        vm((n_t, 8, 128), F32),
        vm((n_t, 8, 128), F32),
        vm((2, 8, 128), F32),
        vm((n_dp, 2, 8, 128), F32),
        vm((width, HW), BF16),
        vm((width, HD), BF16),
        vm((width, HW), BF16),
        vm((width, HD), BF16),
        vm((n_dp, dp_rows, HW), BF16),
        vm((n_dp, dp_rows, HD), BF16),
        vm((n_dp, dp_rows, HW), BF16),
        vm((n_dp, dp_rows, HD), BF16),
        dma((10,)),
        dma((1,)),
        dma((1,)),
        dma((4,)),
        dma((4,)),
        dma((n_t,)),
        dma((n_t,)),
        dma((n_dp,)),
        dma((n_dp,)),
        dma((images, 2 * n_x)),
        dma((images, 2 * n_x)),
        dma((images, 2 * n_x)),
        dma((images, 2 * n_x)),
        dma((images, 2 * n_x)),
        dma((images, 2 * n_x)),
        dma((n_t,)),
        dma((n_t,)),
        dma((2,)),
        dma((2,)),
        dma((n_dp,)),
        dma((n_dp,)),
        dma((n_dp,)),
        dma((n_dp,)),
        dma((n_dp,)),
        dma((n_dp,)),
    ]
    any_spec = pl.BlockSpec(memory_space=pl.ANY)
    smem_spec = pl.BlockSpec(memory_space=pltpu.SMEM)
    vmem_spec = pl.BlockSpec(memory_space=pltpu.VMEM)
    return pl.pallas_call(
        kernel,
        out_shape=(
            jax.ShapeDtypeStruct((dp_rows, HW), F32),
            jax.ShapeDtypeStruct((HD, dp_rows), F32),
            jax.ShapeDtypeStruct((3, dp_rows, HD), F32),
        ),
        in_specs=[smem_spec] * 4 + [any_spec] * 10,
        out_specs=(vmem_spec,) * 3,
        scratch_shapes=scratch,
        compiler_params=pltpu.CompilerParams(
            collective_id=0, has_side_effects=True, vmem_limit_bytes=60 * 1024 * 1024
        ),
        name="step",
    )


def pass_on(*refs):
    half = len(refs) // 2
    for src, dst in zip(refs[:half], refs[half:]):
        dst[...] = src[...]


def local(
    noisy,
    labels,
    tsteps,
    guide_index,
    class_table,
    time_table,
    guide_table,
    guide_weights,
    teacher_qkv,
    teacher_out,
    teacher_ada,
    student_qkv,
    student_out,
    student_ada,
):
    samples, seq_len, _ = noisy.shape
    n_t = lax.axis_size("tensor")
    n_dp = lax.axis_size("dp")
    norm_scale = 1.0 / math.sqrt(samples * n_dp * seq_len)
    step = make_kernel(n_t, n_dp, samples, seq_len, norm_scale)
    grads = step(
        labels, tsteps, guide_index, guide_weights,
        jnp.swapaxes(noisy, 1, 2), class_table, time_table, guide_table,
        teacher_qkv.T, student_qkv.T, teacher_out, student_out,
        jnp.swapaxes(teacher_ada, 1, 2), jnp.swapaxes(student_ada, 1, 2),
    )
    return pl.pallas_call(
        pass_on,
        out_shape=tuple(jax.ShapeDtypeStruct(g.shape, g.dtype) for g in grads),
        name="pass_on",
    )(*grads)


def solution(mesh):
    return jax.shard_map(
        local,
        mesh=mesh,
        in_specs=(
            P("dp", None, "tensor"),
            P("dp"),
            P("dp"),
            P("dp"),
            P(),
            P(),
            P(),
            P(),
            P(None, "tensor"),
            P("tensor", None),
            P(None, None, "tensor"),
            P(None, "tensor"),
            P("tensor", None),
            P(None, None, "tensor"),
        ),
        out_specs=(P("dp", "tensor"), P("tensor", "dp"), P(None, "dp", "tensor")),
        check_vma=False,
    )
```

time: 150 us -> 128 us (0.85); the launches traced: 148 us -> 128 us
  local copies, waits for them, and re-layouts: 14 us -> 0 us
  matrix products: 4.82 us -> 0 us
  other arithmetic: 4.26 us -> 0 us
  Pallas kernels: 124 us -> 127 us
    unnamed x19 -> x0, local copies, waits for them, and re-layouts: 6.1 us -> none
    dot_general x6 -> x0, matrix products: 4.82 us -> none  [the longest x2 1.58 us: lookup_rows(): return jnp.dot(one_hot, table_rows, preferred_element_type=F32)]
    pallas_call x1 -> x2, Pallas kernels: 124 us -> 127 us  [the longest x1 126 us: local(): step(labels, tsteps, guide_index, guide_weights, jnp.swapaxes(noisy, 1, 2...]
    div x2 -> x0, local copies, waits for them, and re-layouts: 2.72 us -> none  [the longest x1 1.9 us: local(): null_act = jax.nn.silu(null_embed).astype(BF16)]
    slice x3 -> x0, local copies, waits for them, and re-layouts: 2.24 us -> none  [the longest x1 1.14 us: local(): act_rows[:, :, :samples].astype(F32)]
where the time goes in v3:
time: 128 us
  Pallas kernels  127 us (99%)
    pallas_call x1, Pallas kernels, local(): step(labels, tsteps, guide_index, guide_weights, jnp.swapaxes(noisy, 1, 2...  126 us

profile of v3, /device:TPU:1, one launch (start us, length us, event | category | flops | bytes accessed | tf_op | source)
XLA Modules:
  0.0 128.0 jit_solution(3513277633782700113)
XLA Ops:
  0.6 125.6 %step.1 = (f32[144,216]{1,0:T(8,128)}, f32[72,144]{1,0:T(8,128)}, f32[3,144,72]{2,1,0:T(8,128)}) custom-call(s32[8]{0:T(128)} %labels.1, s32[8]{0:T(128)} %tsteps.1, s32[8]{0:T(128)} %guides.1, f32[32]{0:T(128)} %strengths.1, bf16[8,72,256]{2,1,0:T(8,128)(2,1)} %bitcast.9, bf16[1001,1152]{1,0:T(8,128)(2,1)} %tab_c.1, bf16[1000,1152]{1,0:T(8,128)(2,1)} %tab_t.1, ...), custom_call_target="tpu_custom_call" | custom-call | tf_op jit(solution)/shard_map/step/pallas_call | solution.py:791
  126.2 1.8 %pass_on.1 = (f32[144,216]{1,0:T(8,128)}, f32[72,144]{1,0:T(8,128)}, f32[3,144,72]{2,1,0:T(8,128)}) custom-call(f32[144,216]{1,0:T(8,128)} %get-tuple-element.6.refs_0_, f32[72,144]{1,0:T(8,128)} %get-tuple-element.7.refs_1_, f32[3,144,72]{2,1,0:T(8,128)} %get-tuple-element.8.refs_2_), custom_call_target="tpu_custom_call" | custom-call | tf_op jit(solution)/shard_map/pass_on/pallas_call | solution.py:797

commit v4 on v3

--- a/solution.py
+++ b/solution.py
@@ -16,6 +16,24 @@
 MESH = pl.DeviceIdType.MESH
 SPLIT = 40
 
+NOISY = (True, True, True, True)
+COT = (True, False, False, True)
+FORWARD = {
+    (0, 2): (("n_pass", 2), ("n_start", 3)),
+    (1, 1): (("n_pass", 3),),
+    (2, 2): (("s_pass", 0),),
+    (3, 1): (("s_end", 0),),
+    (3, 2): (("s_pass", 1),),
+    (3, 4): (("c_pass", 0), ("s_end", 1)),
+}
+BACKWARD = {
+    (0, 0): (("s_pass", 2),),
+    (0, 1): (("c_pass", 1),),
+    (0, 2): (("s_end", 2), ("s_pass", 3)),
+    (1, 1): (("c_pass", 2), ("s_end", 3)),
+    (1, 2): (("c_pass", 3),),
+}
+
 
 def dot(a, b, ca, cb):
     return lax.dot_general(a, b, (((ca,), (cb,)), ((), ())), preferred_element_type=F32)
@@ -42,10 +60,10 @@
         wq_g, wo_g, wq_cat, wq_tr, wo_cat, wo_tr,
         normed, mod_s, mod_t, mixed, mixed_s, proj_s, prob, qkv_s,
         part, rs_in, cot, gp, gqkv, acc_q, acc_o, gmod, gm_send, gm_in, gm_sum, gm_all,
-        pair_q, pair_o, pair_q_in, pair_o_in, dp_q, dp_o, dp_q_in, dp_o_in,
+        pair, pair_in, dp_sum, dp_in,
         l_sem, s_n, r_n, s_w, r_w, s_mod, r_mod, s_act, r_act,
         s_ag, r_ag, s_rs, r_rs, s_c, r_c, s_gm, r_gm, s_pair, r_pair,
-        s_dq, r_dq, s_do, r_do, s_gd, r_gd,
+        s_dq, r_dq, s_gd, r_gd,
     ):
         t = lax.axis_index("tensor")
         j = lax.axis_index("dp")
@@ -84,8 +102,6 @@
             pl.semaphore_signal(
                 barrier, inc=1, device_id={"dp": lax.rem(j + d, n_dp)}, device_id_type=MESH
             )
-        pl.semaphore_wait(barrier, n_t + n_dp - 2)
-
         def to_tensor(src, dst, ss, rs, peer):
             return pltpu.make_async_remote_copy(
                 src_ref=src, dst_ref=dst, send_sem=ss, recv_sem=rs,
@@ -136,40 +152,22 @@
                 )
             return first, second, first[:ahead]
 
-        def by_parity(i, even, odd):
-            @pl.when(lax.rem(i, 2) == 0)
-            def _():
-                even()
-
-            @pl.when(lax.rem(i, 2) == 1)
-            def _():
-                odd()
-
-        def gather_start(buf, i, ss, rs):
-            def run(form):
-                for copy in form(buf, i, ss, rs)[0]:
-                    copy.start()
-
-            by_parity(i, lambda: run(gather_z), lambda: run(gather_x))
-
-        def gather_pass(buf, i, ss, rs):
-            def run(form):
-                _, second, needed = form(buf, i, ss, rs)
-                for copy in needed:
+        def gather_start(buf, i, ss, rs, z_first):
+            for copy in (gather_z if z_first else gather_x)(buf, i, ss, rs)[0]:
+                copy.start()
+
+        def gather_pass(buf, i, ss, rs, z_first):
+            _, second, needed = (gather_z if z_first else gather_x)(buf, i, ss, rs)
+            for copy in needed:
+                copy.wait_recv()
+            for copy in second:
+                copy.start()
+
+        def gather_end(buf, i, ss, rs, z_first):
+            first, second, needed = (gather_z if z_first else gather_x)(buf, i, ss, rs)
+            for copy in first + second:
+                if not any(copy is other for other in needed):
                     copy.wait_recv()
-                for copy in second:
-                    copy.start()
-
-            by_parity(i, lambda: run(gather_z), lambda: run(gather_x))
-
-        def gather_end(buf, i, ss, rs):
-            def run(form):
-                first, second, needed = form(buf, i, ss, rs)
-                for copy in first + second:
-                    if not any(copy is other for other in needed):
-                        copy.wait_recv()
-
-            by_parity(i, lambda: run(gather_z), lambda: run(gather_x))
 
         def sum_z(i):
             first = [
@@ -188,72 +186,29 @@
             ]
             return first, second
 
-        def sum_x(i):
-            first = [
-                to_tensor(
-                    part.at[i, pl.ds(2 * lax.rem(x + d, n_x), 2)], rs_in.at[i, pl.ds(2 * d, 2)],
-                    s_rs.at[i, d], r_rs.at[i, d], device_of(x_chip(d)),
-                )
-                for d in range(1, n_x)
-            ]
-            second = [
-                to_tensor(
-                    part.at[i, chip_z], rs_in.at[i, 0], s_rs.at[i, 0], r_rs.at[i, 0],
-                    device_of(chip_z),
-                )
-            ]
-            return first, second
-
         def sum_start(i):
-            def run(form):
-                for copy in form(i)[0]:
-                    copy.start()
-
-            by_parity(i, lambda: run(sum_z), lambda: run(sum_x))
+            for copy in sum_z(i)[0]:
+                copy.start()
 
         def sum_pass(i):
-            def even():
-                first, second = sum_z(i)
-                for copy in first:
-                    copy.wait_recv()
-                for d in range(1, n_x):
-                    e = lax.rem(x + d, n_x)
-                    total = part[i, 2 * e + z].astype(F32) + rs_in[i, e].astype(F32)
-                    part[i, 2 * e + z] = total.astype(BF16)
-                for copy in second:
-                    copy.start()
-
-            def odd():
-                first, second = sum_x(i)
-                for copy in first:
-                    copy.wait_recv()
-                total = part[i, chip_z].astype(F32)
-                for d in range(1, n_x):
-                    total = total + rs_in[i, 2 * d + 1 - z].astype(F32)
-                part[i, chip_z] = total.astype(BF16)
-                for copy in second:
-                    copy.start()
-
-            by_parity(i, even, odd)
+            first, second = sum_z(i)
+            for copy in first:
+                copy.wait_recv()
+            for d in range(1, n_x):
+                e = lax.rem(x + d, n_x)
+                total = part[i, 2 * e + z].astype(F32) + rs_in[i, e].astype(F32)
+                part[i, 2 * e + z] = total.astype(BF16)
+            for copy in second:
+                copy.start()
 
         def sum_end(i):
-            def even():
-                for copy in sum_z(i)[1]:
-                    copy.wait_recv()
-                total = part[i, chip].astype(F32) + rs_in[i, x].astype(F32)
-                for d in range(1, n_x):
-                    total = total + rs_in[i, n_x + d].astype(F32)
-                cot[i, chip] = total.astype(BF16)
-
-            def odd():
-                for copy in sum_x(i)[1]:
-                    copy.wait_recv()
-                total = part[i, chip].astype(F32) + rs_in[i, 0].astype(F32)
-                for d in range(1, n_x):
-                    total = total + rs_in[i, 2 * d + z].astype(F32)
-                cot[i, chip] = total.astype(BF16)
-
-            by_parity(i, even, odd)
+            for copy in sum_z(i)[1]:
+                copy.wait_recv()
+            total = part[i, chip].astype(F32) + rs_in[i, x].astype(F32)
+            for d in range(1, n_x):
+                total = total + rs_in[i, n_x + d].astype(F32)
+            cot[i, chip] = total.astype(BF16)
+            gather_start(cot, i, s_c, r_c, COT[i])
 
         mate_noisy = to_tensor(
             noisy.at[pl.ds(images * mate, images)], noisy_p.at[core], s_n.at[0], r_n.at[0], mate_t
@@ -264,18 +219,18 @@
             to_tensor(wo_t, wo_g.at[0, core], s_w.at[2], r_w.at[2], mate_t),
             to_tensor(wo_s, wo_g.at[1, core], s_w.at[3], r_w.at[3], mate_t),
         ]
-        mate_noisy.start()
-        for copy in w_copies:
-            copy.start()
-        own_noisy.wait()
-        mate_noisy.wait_recv()
-        for i in range(images):
-            both = jnp.concatenate(
-                [noisy_p[0, i].astype(F32), noisy_p[1, i].astype(F32)], axis=0
-            )
-            noisy_g[i, chip] = both.astype(BF16)
-        for i in range(min(2, images)):
-            gather_start(noisy_g, i, s_ag, r_ag)
+        def mod_copy(d):
+            peer = lax.rem(t + d, n_t)
+            return to_tensor(
+                mods.at[lax.rem(peer, 2)], mod_g.at[t], s_mod.at[d], r_mod.at[d], peer
+            )
+
+        def act_copy(d):
+            peer = lax.rem(j + d, n_dp)
+            return to_dp(
+                acts.at[pl.ds(pl.multiple_of(peer * dp_rows, 16), dp_rows)], act_g.at[j],
+                s_act.at[d], r_act.at[d], peer,
+            )
 
         for copy in loads[:5]:
             copy.wait()
@@ -339,28 +294,28 @@
             )
             mods[kk] = (half[:SPLIT] + low).astype(BF16)
 
-        def mod_copy(d):
-            peer = lax.rem(t + d, n_t)
-            return to_tensor(
-                mods.at[lax.rem(peer, 2)], mod_g.at[t], s_mod.at[d], r_mod.at[d], peer
-            )
-
-        def act_copy(d):
-            peer = lax.rem(j + d, n_dp)
-            return to_dp(
-                acts.at[pl.ds(pl.multiple_of(peer * dp_rows, 16), dp_rows)], act_g.at[j],
-                s_act.at[d], r_act.at[d], peer,
-            )
-
+        pl.semaphore_wait(barrier, n_t + n_dp - 2)
+        mate_noisy.start()
         for d in range(1, n_t):
             mod_copy(d).start()
-        gather_pass(noisy_g, 0, s_ag, r_ag)
-        if images > 2:
-            gather_start(noisy_g, 2, s_ag, r_ag)
+        own_noisy.wait()
+        mate_noisy.wait_recv()
+        for i in range(images):
+            both = jnp.concatenate(
+                [noisy_p[0, i].astype(F32), noisy_p[1, i].astype(F32)], axis=0
+            )
+            noisy_g[i, chip] = both.astype(BF16)
+            if i == 0:
+                gather_start(noisy_g, 0, s_ag, r_ag, NOISY[0])
+        for copy in w_copies:
+            copy.start()
+        mod_g[t] = mods[core]
+        act_g[j] = acts[pl.ds(pl.multiple_of(j * dp_rows, 16), dp_rows), :]
+
+        gather_pass(noisy_g, 0, s_ag, r_ag, NOISY[0])
+        gather_start(noisy_g, 1, s_ag, r_ag, NOISY[1])
         for d in range(1, n_dp):
             act_copy(d).start()
-        mod_g[t] = mods[core]
-        act_g[j] = acts[pl.ds(pl.multiple_of(j * dp_rows, 16), dp_rows), :]
 
         for copy in loads[5:]:
             copy.wait()
@@ -378,9 +333,8 @@
         acc_q[...] = jnp.zeros_like(acc_q)
         acc_o[...] = jnp.zeros_like(acc_o)
         gmod[...] = jnp.zeros_like(gmod)
-        gather_pass(noisy_g, 1, s_ag, r_ag)
-        if images > 3:
-            gather_start(noisy_g, 3, s_ag, r_ag)
+        gather_pass(noisy_g, 1, s_ag, r_ag, NOISY[1])
+        gather_start(noisy_g, 2, s_ag, r_ag, NOISY[2])
 
         for d in range(1, n_t):
             mod_copy(d).wait_recv()
@@ -403,7 +357,12 @@
             return p, dot(v, p.astype(BF16), 1, 0)[:HD]
 
         def forward_in(i):
-            gather_end(noisy_g, i, s_ag, r_ag)
+            for q in range(images):
+
+                @pl.when(i == q)
+                def _():
+                    gather_end(noisy_g, q, s_ag, r_ag, NOISY[q])
+
             total = jnp.zeros((1, seq), F32)
             square = jnp.zeros((1, seq), F32)
             for c in range(chips):
@@ -458,7 +417,12 @@
             sum_start(i)
 
         def backward_in(i):
-            gather_end(cot, i, s_c, r_c)
+            for q in range(images):
+
+                @pl.when(i == q)
+                def _():
+                    gather_end(cot, q, s_c, r_c, COT[q])
+
             grads = []
             for c in range(chips):
                 rows = slice(block * c, block * (c + 1))
@@ -503,82 +467,74 @@
                 lane == 4 + i, jnp.concatenate(scales, axis=0), 0.0
             )
 
+        stages = {
+            "n_start": lambda q: gather_start(noisy_g, q, s_ag, r_ag, NOISY[q]),
+            "n_pass": lambda q: gather_pass(noisy_g, q, s_ag, r_ag, NOISY[q]),
+            "s_pass": sum_pass,
+            "s_end": sum_end,
+            "c_pass": lambda q: gather_pass(cot, q, s_c, r_c, COT[q]),
+        }
+
+        def at(i, point, table):
+            for (step, where), names in table.items():
+                if where == point:
+
+                    @pl.when(i == step)
+                    def _():
+                        for name, q in names:
+                            stages[name](q)
+
         def forward_step(i, carry):
             forward_in(i)
-
-            @pl.when(i < images - 2)
-            def _():
-                gather_pass(noisy_g, i + 2, s_ag, r_ag)
-
+            at(i, 1, FORWARD)
             forward_model(i, 0)
-
-            @pl.when(i > 0)
-            def _():
-                sum_pass(i - 1)
-
+            at(i, 2, FORWARD)
             forward_model(i, 1)
-
-            @pl.when(i > 1)
-            def _():
-                gather_pass(cot, i - 2, s_c, r_c)
-
+            at(i, 3, FORWARD)
             forward_model(i, 2)
-
-            @pl.when(i > 0)
-            def _():
-                sum_end(i - 1)
-                gather_start(cot, i - 1, s_c, r_c)
-
+            at(i, 4, FORWARD)
             forward_out(i)
             return carry
 
         lax.fori_loop(0, images, forward_step, 0)
-        if images > 1:
-            gather_pass(cot, images - 2, s_c, r_c)
-        sum_pass(images - 1)
-
-        def backward_step(i, carry):
-            backward_in(i)
-
-            @pl.when(i == 0)
-            def _():
-                sum_end(images - 1)
-                gather_start(cot, images - 1, s_c, r_c)
-
-            backward_out(i)
-
-            @pl.when(i == 0)
-            def _():
-                gather_pass(cot, images - 1, s_c, r_c)
-
-            return carry
-
-        lax.fori_loop(0, images, backward_step, 0)
 
         def gm_copy(d):
             peer = lax.rem(t + d, n_t)
             return to_tensor(gm_send.at[peer], gm_in.at[t], s_gm.at[d], r_gm.at[d], peer)
 
-        pair_copies = [
-            to_tensor(pair_q, pair_q_in, s_pair.at[0], r_pair.at[0], mate_t),
-            to_tensor(pair_o, pair_o_in, s_pair.at[1], r_pair.at[1], mate_t),
-        ]
-
-        def dp_copies(d):
+        def pair_copy(s):
+            return to_tensor(pair.at[s], pair_in.at[s], s_pair.at[s], r_pair.at[s], mate_t)
+
+        def dp_copy(d):
             peer = lax.rem(j + d, n_dp)
-            return [
-                to_dp(dp_q.at[peer], dp_q_in.at[j], s_dq.at[d], r_dq.at[d], peer),
-                to_dp(dp_o.at[peer], dp_o_in.at[j], s_do.at[d], r_do.at[d], peer),
-            ]
+            return to_dp(dp_sum.at[peer], dp_in.at[j], s_dq.at[d], r_dq.at[d], peer)
 
         def gd_copy(d):
             peer = lax.rem(j + d, n_dp)
             return to_dp(gm_sum, gm_all.at[j], s_gd.at[d], r_gd.at[d], peer)
 
-        pair_q[...] = acc_q[mate].astype(BF16)
-        pair_o[...] = acc_o[mate].astype(BF16)
-        for copy in pair_copies:
-            copy.start()
+        def chunk(s):
+            return pl.ds(pl.multiple_of(s * dp_rows, 16), dp_rows)
+
+        def backward_step(i, carry):
+            at(i, 0, BACKWARD)
+            backward_in(i)
+            at(i, 1, BACKWARD)
+
+            @pl.when(i == images - 1)
+            def _():
+                for d in range(1, n_dp + 1):
+                    s = lax.rem(j + d, n_dp)
+                    pair[s, :, 0:HW] = acc_q[mate, chunk(s), :].astype(BF16)
+                    pair[s, :, 256 : 256 + HD] = acc_o[mate, chunk(s), :].astype(BF16)
+                    pair_copy(s).start()
+
+            backward_out(i)
+            at(i, 2, BACKWARD)
+            return carry
+
+        lax.fori_loop(0, images, backward_step, 0)
+
         for src in range(n_t):
             packed = gmod[HD * src : HD * src + 8, :]
             for g in range(1, groups):
@@ -588,15 +544,17 @@
         for d in range(1, n_t):
             gm_copy(d).start()
         gm_in[t] = gm_send[t]
-        for copy in pair_copies:
-            copy.wait_recv()
-        for s in range(n_dp):
-            rows = slice(dp_rows * s, dp_rows * (s + 1))
-            dp_q[s] = (acc_q[core, rows, :] + pair_q_in[rows, :].astype(F32)).astype(BF16)
-            dp_o[s] = (acc_o[core, rows, :] + pair_o_in[rows, :].astype(F32)).astype(BF16)
-        for d in range(1, n_dp):
-            for copy in dp_copies(d):
-                copy.start()
+        for d in range(1, n_dp + 1):
+            s = lax.rem(j + d, n_dp)
+            pair_copy(s).wait_recv()
+            dp_sum[s, :, 0:HW] = (
+                acc_q[core, chunk(s), :] + pair_in[s, :, 0:HW].astype(F32)
+            ).astype(BF16)
+            dp_sum[s, :, 256 : 256 + HD] = (
+                acc_o[core, chunk(s), :] + pair_in[s, :, 256 : 256 + HD].astype(F32)
+            ).astype(BF16)
+            if d < n_dp:
+                dp_copy(d).start()
         for d in range(1, n_t):
             gm_copy(d).wait_recv()
         for kk in range(2):
@@ -613,15 +571,14 @@
         for s in range(1, n_dp):
             rows_act = rows_act + pltpu.roll(act_g[s].astype(F32), samples * s, 1)
 
-        total_q = dp_q[j].astype(F32)
-        total_o = dp_o[j].astype(F32)
+        total_q = dp_sum[j, :, 0:HW].astype(F32)
+        total_o = dp_sum[j, :, 256 : 256 + HD].astype(F32)
         for d in range(1, n_dp):
-            for copy in dp_copies(d):
-                copy.wait_recv()
+            dp_copy(d).wait_recv()
         for d in range(1, n_dp):
             src = lax.rem(j + d, n_dp)
-            total_q = total_q + dp_q_in[src].astype(F32)
-            total_o = total_o + dp_o_in[src].astype(F32)
+            total_q = total_q + dp_in[src, :, 0:HW].astype(F32)
+            total_o = total_o + dp_in[src, :, 256 : 256 + HD].astype(F32)
         gq_out[...] = total_q
         go_out[...] = jnp.transpose(total_o)
 
@@ -647,23 +604,24 @@
             )
 
         mate_noisy.wait_send()
-        for copy in w_copies + pair_copies:
+        for copy in w_copies:
             copy.wait_send()
+        for s in range(n_dp):
+            pair_copy(s).wait_send()
         for d in range(1, n_t):
             mod_copy(d).wait_send()
             gm_copy(d).wait_send()
         for d in range(1, n_dp):
             act_copy(d).wait_send()
             gd_copy(d).wait_send()
-            for copy in dp_copies(d):
-                copy.wait_send()
+            dp_copy(d).wait_send()
         for i in range(images):
-            form = gather_z if i % 2 == 0 else gather_x
-            sums = sum_z(i) if i % 2 == 0 else sum_x(i)
+            of_noisy = gather_z if NOISY[i] else gather_x
+            of_cot = gather_z if COT[i] else gather_x
             for copy in (
-                sum(form(noisy_g, i, s_ag, r_ag)[:2], [])
-                + sum(form(cot, i, s_c, r_c)[:2], [])
-                + sum(sums, [])
+                sum(of_noisy(noisy_g, i, s_ag, r_ag)[:2], [])
+                + sum(of_cot(cot, i, s_c, r_c)[:2], [])
+                + sum(sum_z(i), [])
             ):
                 copy.wait_send()
 
@@ -707,14 +665,10 @@
         vm((n_t, 8, 128), F32),
         vm((2, 8, 128), F32),
         vm((n_dp, 2, 8, 128), F32),
-        vm((width, HW), BF16),
-        vm((width, HD), BF16),
-        vm((width, HW), BF16),
-        vm((width, HD), BF16),
-        vm((n_dp, dp_rows, HW), BF16),
-        vm((n_dp, dp_rows, HD), BF16),
-        vm((n_dp, dp_rows, HW), BF16),
-        vm((n_dp, dp_rows, HD), BF16),
+        vm((n_dp, dp_rows, 384), BF16),
+        vm((n_dp, dp_rows, 384), BF16),
+        vm((n_dp, dp_rows, 384), BF16),
+        vm((n_dp, dp_rows, 384), BF16),
         dma((10,)),
         dma((1,)),
         dma((1,)),
@@ -732,8 +686,6 @@
         dma((images, 2 * n_x)),
         dma((n_t,)),
         dma((n_t,)),
-        dma((2,)),
-        dma((2,)),
         dma((n_dp,)),
         dma((n_dp,)),
         dma((n_dp,)),

time: 128 us -> 104 us (0.81)
  Pallas kernels: 127 us -> 103 us
    pallas_call x1, Pallas kernels: 126 us -> 101 us  [local(): step(labels, tsteps, guide_index, guide_weights, jnp.swapaxes(noisy, 1, 2...]
where the time goes in v4:
time: 104 us; the launch traced here: 103 us
  Pallas kernels  103 us (99%)
    pallas_call x1, Pallas kernels, local(): step(labels, tsteps, guide_index, guide_weights, jnp.swapaxes(noisy, 1, 2...  101 us

profile of v4, /device:TPU:1, one launch (start us, length us, event | category | flops | bytes accessed | tf_op | source)
XLA Modules:
  0.0 103.3 jit_solution(17016428044782840940)
XLA Ops:
  0.6 100.9 %step.1 = (f32[144,216]{1,0:T(8,128)}, f32[72,144]{1,0:T(8,128)}, f32[3,144,72]{2,1,0:T(8,128)}) custom-call(s32[8]{0:T(128)} %labels.1, s32[8]{0:T(128)} %tsteps.1, s32[8]{0:T(128)} %guides.1, f32[32]{0:T(128)} %strengths.1, bf16[8,72,256]{2,1,0:T(8,128)(2,1)} %bitcast.9, bf16[1001,1152]{1,0:T(8,128)(2,1)} %tab_c.1, bf16[1000,1152]{1,0:T(8,128)(2,1)} %tab_t.1, ...), custom_call_target="tpu_custom_call" | custom-call | tf_op jit(solution)/shard_map/step/pallas_call | solution.py:743
  101.5 1.8 %pass_on.1 = (f32[144,216]{1,0:T(8,128)}, f32[72,144]{1,0:T(8,128)}, f32[3,144,72]{2,1,0:T(8,128)}) custom-call(f32[144,216]{1,0:T(8,128)} %get-tuple-element.6.refs_0_, f32[72,144]{1,0:T(8,128)} %get-tuple-element.7.refs_1_, f32[3,144,72]{2,1,0:T(8,128)} %get-tuple-element.8.refs_2_), custom_call_target="tpu_custom_call" | custom-call | tf_op jit(solution)/shard_map/pass_on/pallas_call | solution.py:749

commit v5 on v4

--- a/solution.py
+++ b/solution.py
@@ -10,6 +10,7 @@
 HD = 72
 HW = 3 * HD
 HP = 80
+FREE = 256 - HW
 norm_eps = 1e-06
 F32 = jnp.float32
 BF16 = jnp.bfloat16
@@ -19,8 +20,9 @@
 NOISY = (True, True, True, True)
 COT = (True, False, False, True)
 FORWARD = {
-    (0, 2): (("n_pass", 2), ("n_start", 3)),
-    (1, 1): (("n_pass", 3),),
+    (0, 1): (("n_pass", 1), ("n_start", 2)),
+    (0, 4): (("n_pass", 2), ("n_start", 3)),
+    (1, 2): (("n_pass", 3),),
     (2, 2): (("s_pass", 0),),
     (3, 1): (("s_end", 0),),
     (3, 2): (("s_pass", 1),),
@@ -56,14 +58,14 @@
         labels, tsteps, guides, strengths,
         noisy, tab_c, tab_t, tab_g, wq_t, wq_s, wo_t, wo_s, ada_t, ada_s,
         gq_out, go_out, ga_out,
-        noisy_p, noisy_g, c_tab, t_tab, g_tab, a_tab, mods, mod_g, mod_i, acts, act_g,
+        noisy_p, noisy_v, noisy_g, c_tab, t_tab, g_tab, a_tab, mods, mod_g, mod_i, acts, act_g,
         wq_g, wo_g, wq_cat, wq_tr, wo_cat, wo_tr,
         normed, mod_s, mod_t, mixed, mixed_s, proj_s, prob, qkv_s,
         part, rs_in, cot, gp, gqkv, acc_q, acc_o, gmod, gm_send, gm_in, gm_sum, gm_all,
-        pair, pair_in, dp_sum, dp_in,
+        pair, pair_in, dp_sum, dp_in, dp_ex, dp_ex_in,
         l_sem, s_n, r_n, s_w, r_w, s_mod, r_mod, s_act, r_act,
         s_ag, r_ag, s_rs, r_rs, s_c, r_c, s_gm, r_gm, s_pair, r_pair,
-        s_dq, r_dq, s_gd, r_gd,
+        s_dq, r_dq, s_do, r_do, s_gd, r_gd,
     ):
         t = lax.axis_index("tensor")
         j = lax.axis_index("dp")
@@ -86,9 +88,7 @@
             pltpu.make_async_copy(wo_t, wo_g.at[0, core], l_sem.at[7]),
             pltpu.make_async_copy(wo_s, wo_g.at[1, core], l_sem.at[8]),
         ]
-        own_noisy = pltpu.make_async_copy(
-            noisy.at[pl.ds(images * core, images)], noisy_p.at[core], l_sem.at[9]
-        )
+        own_noisy = pltpu.make_async_copy(noisy, noisy_v, l_sem.at[9])
         own_noisy.start()
         for copy in loads:
             copy.start()
@@ -210,9 +210,10 @@
             cot[i, chip] = total.astype(BF16)
             gather_start(cot, i, s_c, r_c, COT[i])
 
-        mate_noisy = to_tensor(
-            noisy.at[pl.ds(images * mate, images)], noisy_p.at[core], s_n.at[0], r_n.at[0], mate_t
-        )
+        mate_noisy = [
+            to_tensor(noisy_v.at[images * mate + i], noisy_p.at[i], s_n.at[i], r_n.at[i], mate_t)
+            for i in range(images)
+        ]
         w_copies = [
             to_tensor(wq_t, wq_g.at[0, core], s_w.at[0], r_w.at[0], mate_t),
             to_tensor(wq_s, wq_g.at[1, core], s_w.at[1], r_w.at[1], mate_t),
@@ -295,16 +296,18 @@
             mods[kk] = (half[:SPLIT] + low).astype(BF16)
 
         pl.semaphore_wait(barrier, n_t + n_dp - 2)
-        mate_noisy.start()
+        own_noisy.wait()
+        for copy in mate_noisy:
+            copy.start()
         for d in range(1, n_t):
             mod_copy(d).start()
-        own_noisy.wait()
-        mate_noisy.wait_recv()
         for i in range(images):
-            both = jnp.concatenate(
-                [noisy_p[0, i].astype(F32), noisy_p[1, i].astype(F32)], axis=0
-            )
-            noisy_g[i, chip] = both.astype(BF16)
+            mate_noisy[i].wait_recv()
+            own = noisy_v[images * core + i].astype(F32)
+            other = noisy_p[i].astype(F32)
+            first = jnp.where(core == 0, own, other)
+            second = jnp.where(core == 0, other, own)
+            noisy_g[i, chip] = jnp.concatenate([first, second], axis=0).astype(BF16)
             if i == 0:
                 gather_start(noisy_g, 0, s_ag, r_ag, NOISY[0])
         for copy in w_copies:
@@ -333,8 +336,6 @@
         acc_q[...] = jnp.zeros_like(acc_q)
         acc_o[...] = jnp.zeros_like(acc_o)
         gmod[...] = jnp.zeros_like(gmod)
-        gather_pass(noisy_g, 1, s_ag, r_ag, NOISY[1])
-        gather_start(noisy_g, 2, s_ag, r_ag, NOISY[2])
 
         for d in range(1, n_t):
             mod_copy(d).wait_recv()
@@ -438,7 +439,7 @@
             acts_grad = []
             for h in range(2):
                 low = padded(grad_mixed[HD * h : HD * (h + 1)])
-                acc_o[h] += dot(gp[...], mixed_s[i, h], 1, 1)
+                acc_o[h, :, 0:HD] += dot(gp[...], mixed_s[i, h], 1, 1)
                 q, k, v = (qkv_s[i, h, e] for e in range(3))
                 p = prob[i, h]
                 grad_prob = dot(v, low, 0, 0)
@@ -450,7 +451,7 @@
             gqkv[...] = jnp.concatenate(acts_grad, axis=0).astype(BF16)
             for h in range(2):
                 head = jnp.concatenate(acts_grad[3 * h : 3 * h + 3], axis=0).astype(BF16)
-                acc_q[h] += dot(mod_s[i], head, 1, 1)
+                acc_q[h, :, 0:HW] += dot(mod_s[i], head, 1, 1)
 
         def backward_out(i):
             shifts = []
@@ -505,9 +506,15 @@
         def pair_copy(s):
             return to_tensor(pair.at[s], pair_in.at[s], s_pair.at[s], r_pair.at[s], mate_t)
 
-        def dp_copy(d):
+        def dp_copies(d):
             peer = lax.rem(j + d, n_dp)
-            return to_dp(dp_sum.at[peer], dp_in.at[j], s_dq.at[d], r_dq.at[d], peer)
+            return [
+                to_dp(dp_sum.at[peer], dp_in.at[j], s_dq.at[d], r_dq.at[d], peer),
+                to_dp(dp_ex.at[peer], dp_ex_in.at[j], s_do.at[d], r_do.at[d], peer),
+            ]
+
+        third = dp_rows // 3
+        early = [d for d in (1, 3, 4, 5) if d < n_dp]
 
         def gd_copy(d):
             peer = lax.rem(j + d, n_dp)
@@ -525,8 +532,8 @@
             def _():
                 for d in range(1, n_dp + 1):
                     s = lax.rem(j + d, n_dp)
-                    pair[s, :, 0:HW] = acc_q[mate, chunk(s), :].astype(BF16)
-                    pair[s, :, 256 : 256 + HD] = acc_o[mate, chunk(s), :].astype(BF16)
+                    pair[s, :, 0:256] = acc_q[mate, chunk(s), :].astype(BF16)
+                    pair[s, :, 256:384] = acc_o[mate, chunk(s), :].astype(BF16)
                     pair_copy(s).start()
 
             backward_out(i)
@@ -547,14 +554,23 @@
         for d in range(1, n_dp + 1):
             s = lax.rem(j + d, n_dp)
             pair_copy(s).wait_recv()
-            dp_sum[s, :, 0:HW] = (
-                acc_q[core, chunk(s), :] + pair_in[s, :, 0:HW].astype(F32)
+            sums_q = acc_q[core, chunk(s), :] + pair_in[s, :, 0:256].astype(F32)
+            sums_o = acc_o[core, chunk(s), :] + pair_in[s, :, 256:384].astype(F32)
+            moved = pltpu.roll(sums_o, 128 - FREE, 1)
+            lane = iota((dp_rows, 128), 1)
+            dp_sum[s, :, 0:128] = sums_q[:, :128].astype(BF16)
+            dp_sum[s, :, 128:256] = (
+                sums_q[:, 128:] + jnp.where(lane >= 128 - FREE, moved, 0.0)
             ).astype(BF16)
-            dp_sum[s, :, 256 : 256 + HD] = (
-                acc_o[core, chunk(s), :] + pair_in[s, :, 256 : 256 + HD].astype(F32)
+            rest = jnp.where(lane < HD - FREE, moved, 0.0)
+            dp_ex[s] = (
+                rest[:third]
+                + pltpu.roll(rest[third : 2 * third], 32, 1)
+                + pltpu.roll(rest[2 * third :], 64, 1)
             ).astype(BF16)
-            if d < n_dp:
-                dp_copy(d).start()
+            if d in early:
+                for copy in dp_copies(d):
+                    copy.start()
         for d in range(1, n_t):
             gm_copy(d).wait_recv()
         for kk in range(2):
@@ -564,6 +580,10 @@
             gm_sum[kk] = total
         for d in range(1, n_dp):
             gd_copy(d).start()
+        for d in range(1, n_dp):
+            if d not in early:
+                for copy in dp_copies(d):
+                    copy.start()
         gm_all[j] = gm_sum[...]
         for d in range(1, n_dp):
             act_copy(d).wait_recv()
@@ -571,16 +591,24 @@
         for s in range(1, n_dp):
             rows_act = rows_act + pltpu.roll(act_g[s].astype(F32), samples * s, 1)
 
-        total_q = dp_sum[j, :, 0:HW].astype(F32)
-        total_o = dp_sum[j, :, 256 : 256 + HD].astype(F32)
+        total = dp_sum[j].astype(F32)
+        rest = dp_ex[j].astype(F32)
         for d in range(1, n_dp):
-            dp_copy(d).wait_recv()
+            for copy in dp_copies(d):
+                copy.wait_recv()
         for d in range(1, n_dp):
             src = lax.rem(j + d, n_dp)
-            total_q = total_q + dp_in[src, :, 0:HW].astype(F32)
-            total_o = total_o + dp_in[src, :, 256 : 256 + HD].astype(F32)
-        gq_out[...] = total_q
-        go_out[...] = jnp.transpose(total_o)
+            total = total + dp_in[src].astype(F32)
+            rest = rest + dp_ex_in[src].astype(F32)
+        gq_out[...] = total[:, :HW]
+        lane = iota((dp_rows, 128), 1)
+        spread = jnp.concatenate(
+            [rest, pltpu.roll(rest, 128 - 32, 1), pltpu.roll(rest, 128 - 64, 1)], axis=0
+        )
+        total_o = jnp.where(lane >= 128 - FREE, total[:, 128:], 0.0) + jnp.where(
+            lane < HD - FREE, spread, 0.0
+        )
+        go_out[...] = jnp.transpose(pltpu.roll(total_o, FREE, 1))[:HD]
 
         for d in range(1, n_dp):
             gd_copy(d).wait_recv()
@@ -603,8 +631,7 @@
                 precision=lax.Precision.HIGHEST, preferred_element_type=F32,
             )
 
-        mate_noisy.wait_send()
-        for copy in w_copies:
+        for copy in mate_noisy + w_copies:
             copy.wait_send()
         for s in range(n_dp):
             pair_copy(s).wait_send()
@@ -614,7 +641,8 @@
         for d in range(1, n_dp):
             act_copy(d).wait_send()
             gd_copy(d).wait_send()
-            dp_copy(d).wait_send()
+            for copy in dp_copies(d):
+                copy.wait_send()
         for i in range(images):
             of_noisy = gather_z if NOISY[i] else gather_x
             of_cot = gather_z if COT[i] else gather_x
@@ -628,7 +656,8 @@
     vm = pltpu.VMEM
     dma = pltpu.SemaphoreType.DMA
     scratch = [
-        vm((2, images, HD, seq), BF16),
+        vm((images, HD, seq), BF16),
+        vm((samples, HD, seq), BF16),
         vm((images, chips, block, seq), BF16),
         vm((1001, width), BF16),
         vm((1000, width), BF16),
@@ -658,8 +687,8 @@
         vm((images, chips, block, seq), BF16),
         vm((width, seq), BF16),
         vm((2 * HW, seq), BF16),
-        vm((2, width, HW), F32),
-        vm((2, width, HD), F32),
+        vm((2, width, 256), F32),
+        vm((2, width, 128), F32),
         vm((width, 128), F32),
         vm((n_t, 8, 128), F32),
         vm((n_t, 8, 128), F32),
@@ -667,11 +696,13 @@
         vm((n_dp, 2, 8, 128), F32),
         vm((n_dp, dp_rows, 384), BF16),
         vm((n_dp, dp_rows, 384), BF16),
-        vm((n_dp, dp_rows, 384), BF16),
-        vm((n_dp, dp_rows, 384), BF16),
+        vm((n_dp, dp_rows, 256), BF16),
+        vm((n_dp, dp_rows, 256), BF16),
+        vm((n_dp, dp_rows // 3, 128), BF16),
+        vm((n_dp, dp_rows // 3, 128), BF16),
         dma((10,)),
-        dma((1,)),
-        dma((1,)),
+        dma((images,)),
+        dma((images,)),
         dma((4,)),
         dma((4,)),
         dma((n_t,)),
@@ -686,6 +717,8 @@
         dma((images, 2 * n_x)),
         dma((n_t,)),
         dma((n_t,)),
+        dma((n_dp,)),
+        dma((n_dp,)),
         dma((n_dp,)),
         dma((n_dp,)),
         dma((n_dp,)),

time: 104 us -> 102 us (0.981)
  Pallas kernels: 103 us -> 101 us
    pallas_call x1, Pallas kernels: 101 us -> 99.4 us  [local(): step(labels, tsteps, guide_index, guide_weights, jnp.swapaxes(noisy, 1, 2...]
where the time goes in v5:
time: 102 us
  Pallas kernels  101 us (99%)
    pallas_call x1, Pallas kernels, local(): step(labels, tsteps, guide_index, guide_weights, jnp.swapaxes(noisy, 1, 2...  99.4 us

profile of v5, /device:TPU:1, one launch (start us, length us, event | category | flops | bytes accessed | tf_op | source)
XLA Modules:
  0.0 101.9 jit_solution(3095691389814782729)
XLA Ops:
  0.6 99.4 %step.1 = (f32[144,216]{1,0:T(8,128)}, f32[72,144]{1,0:T(8,128)}, f32[3,144,72]{2,1,0:T(8,128)}) custom-call(s32[8]{0:T(128)} %labels.1, s32[8]{0:T(128)} %tsteps.1, s32[8]{0:T(128)} %guides.1, f32[32]{0:T(128)} %strengths.1, bf16[8,72,256]{2,1,0:T(8,128)(2,1)} %bitcast.9, bf16[1001,1152]{1,0:T(8,128)(2,1)} %tab_c.1, bf16[1000,1152]{1,0:T(8,128)(2,1)} %tab_t.1, ...), custom_call_target="tpu_custom_call" | custom-call | tf_op jit(solution)/shard_map/step/pallas_call | solution.py:776
  100.1 1.8 %pass_on.1 = (f32[144,216]{1,0:T(8,128)}, f32[72,144]{1,0:T(8,128)}, f32[3,144,72]{2,1,0:T(8,128)}) custom-call(f32[144,216]{1,0:T(8,128)} %get-tuple-element.6.refs_0_, f32[72,144]{1,0:T(8,128)} %get-tuple-element.7.refs_1_, f32[3,144,72]{2,1,0:T(8,128)} %get-tuple-element.8.refs_2_), custom_call_target="tpu_custom_call" | custom-call | tf_op jit(solution)/shard_map/pass_on/pallas_call | solution.py:782

commit v6 on v5

--- a/solution.py
+++ b/solution.py
@@ -514,7 +514,7 @@
             ]
 
         third = dp_rows // 3
-        early = [d for d in (1, 3, 4, 5) if d < n_dp]
+        early = [d for d in range(1, n_dp)]
 
         def gd_copy(d):
             peer = lax.rem(j + d, n_dp)

time: 102 us -> 101 us (level); the launches traced: 102 us -> 99.5 us
  Pallas kernels: 101 us -> 98.8 us
    pallas_call x1, Pallas kernels: 99.4 us -> 97 us  [local(): step(labels, tsteps, guide_index, guide_weights, jnp.swapaxes(noisy, 1, 2...]
where the time goes in v6:
time: 101 us; the launch traced here: 99.5 us
  Pallas kernels  98.8 us (98%)
    pallas_call x1, Pallas kernels, local(): step(labels, tsteps, guide_index, guide_weights, jnp.swapaxes(noisy, 1, 2...  97 us

profile of v6, /device:TPU:1, one launch (start us, length us, event | category | flops | bytes accessed | tf_op | source)
XLA Modules:
  0.0 99.5 jit_solution(4783648728009216012)
XLA Ops:
  0.6 97.0 %step.1 = (f32[144,216]{1,0:T(8,128)}, f32[72,144]{1,0:T(8,128)}, f32[3,144,72]{2,1,0:T(8,128)}) custom-call(s32[8]{0:T(128)} %labels.1, s32[8]{0:T(128)} %tsteps.1, s32[8]{0:T(128)} %guides.1, f32[32]{0:T(128)} %strengths.1, bf16[8,72,256]{2,1,0:T(8,128)(2,1)} %bitcast.9, bf16[1001,1152]{1,0:T(8,128)(2,1)} %tab_c.1, bf16[1000,1152]{1,0:T(8,128)(2,1)} %tab_t.1, ...), custom_call_target="tpu_custom_call" | custom-call | tf_op jit(solution)/shard_map/step/pallas_call | solution.py:776
  97.7 1.8 %pass_on.1 = (f32[144,216]{1,0:T(8,128)}, f32[72,144]{1,0:T(8,128)}, f32[3,144,72]{2,1,0:T(8,128)}) custom-call(f32[144,216]{1,0:T(8,128)} %get-tuple-element.6.refs_0_, f32[72,144]{1,0:T(8,128)} %get-tuple-element.7.refs_1_, f32[3,144,72]{2,1,0:T(8,128)} %get-tuple-element.8.refs_2_), custom_call_target="tpu_custom_call" | custom-call | tf_op jit(solution)/shard_map/pass_on/pallas_call | solution.py:782

commit v7 on v6

--- a/solution.py
+++ b/solution.py
@@ -515,6 +515,8 @@
 
         third = dp_rows // 3
         early = [d for d in range(1, n_dp)]
+        far = (6, 2, 5, 3, 4, 7, 1)
+        order = [d for d in far if d < n_dp] + [d for d in range(8, n_dp)] + [n_dp]
 
         def gd_copy(d):
             peer = lax.rem(j + d, n_dp)
@@ -530,7 +532,7 @@
 
             @pl.when(i == images - 1)
             def _():
-                for d in range(1, n_dp + 1):
+                for d in order:
                     s = lax.rem(j + d, n_dp)
                     pair[s, :, 0:256] = acc_q[mate, chunk(s), :].astype(BF16)
                     pair[s, :, 256:384] = acc_o[mate, chunk(s), :].astype(BF16)
@@ -551,7 +553,7 @@
         for d in range(1, n_t):
             gm_copy(d).start()
         gm_in[t] = gm_send[t]
-        for d in range(1, n_dp + 1):
+        for d in order:
             s = lax.rem(j + d, n_dp)
             pair_copy(s).wait_recv()
             sums_q = acc_q[core, chunk(s), :] + pair_in[s, :, 0:256].astype(F32)

time: 101 us -> 101 us (level); the launches traced: 99.5 us -> 101 us
  Pallas kernels: 98.8 us -> 101 us
    pallas_call x1, Pallas kernels: 97 us -> 98.9 us  [local(): step(labels, tsteps, guide_index, guide_weights, jnp.swapaxes(noisy, 1, 2...]
where the time goes in v7:
time: 101 us
  Pallas kernels  101 us (100%)
    pallas_call x1, Pallas kernels, local(): step(labels, tsteps, guide_index, guide_weights, jnp.swapaxes(noisy, 1, 2...  98.9 us

profile of v7, /device:TPU:1, one launch (start us, length us, event | category | flops | bytes accessed | tf_op | source)
XLA Modules:
  0.0 101.3 jit_solution(7254160243132742317)
XLA Ops:
  0.6 98.9 %step.1 = (f32[144,216]{1,0:T(8,128)}, f32[72,144]{1,0:T(8,128)}, f32[3,144,72]{2,1,0:T(8,128)}) custom-call(s32[8]{0:T(128)} %labels.1, s32[8]{0:T(128)} %tsteps.1, s32[8]{0:T(128)} %guides.1, f32[32]{0:T(128)} %strengths.1, bf16[8,72,256]{2,1,0:T(8,128)(2,1)} %bitcast.9, bf16[1001,1152]{1,0:T(8,128)(2,1)} %tab_c.1, bf16[1000,1152]{1,0:T(8,128)(2,1)} %tab_t.1, ...), custom_call_target="tpu_custom_call" | custom-call | tf_op jit(solution)/shard_map/step/pallas_call | solution.py:778
  99.5 1.8 %pass_on.1 = (f32[144,216]{1,0:T(8,128)}, f32[72,144]{1,0:T(8,128)}, f32[3,144,72]{2,1,0:T(8,128)}) custom-call(f32[144,216]{1,0:T(8,128)} %get-tuple-element.6.refs_0_, f32[72,144]{1,0:T(8,128)} %get-tuple-element.7.refs_1_, f32[3,144,72]{2,1,0:T(8,128)} %get-tuple-element.8.refs_2_), custom_call_target="tpu_custom_call" | custom-call | tf_op jit(solution)/shard_map/pass_on/pallas_call | solution.py:784
